TPU v7x, 32 devices: a whole 2x2x4 slice. The times are simulated.
32 devices in a mesh: wide: 8 (over y, x, core), narrow: 4 (over z).
Axes of the slice: x: 2, y: 2, z: 4, core: 2. Of those that a mesh axis runs over, the one named last changes fastest.
Arguments:
- left: bfloat16 [32, 32, 256], P('narrow', None, 'wide'), may hold values from -6 to 6
- right: bfloat16 [32, 32, 256], P('wide', None, 'narrow'), may hold values from -6 to 6
- out_weight: bfloat16 [1024, 128], replicated, may hold values from -1 to 1
- out_bias: float32 [128], replicated, may hold values from -3 to 3
- cotangent: bfloat16 [256, 256, 128], P('wide', 'narrow'), may hold values from -0.5 to 0.5
Outputs:
- pair_update: bfloat16 [256, 256, 128], P('wide', 'narrow')
- grad_left: float32 [32, 32, 256], P('narrow', None, 'wide')
- grad_right: float32 [32, 32, 256], P('wide', None, 'narrow')
All inputs are finite; a program needn't handle non-finite values.
Results may differ from a plain program's by a relative error of at most 0.0045.
Values may be sent and summed in bfloat16 or wider, within the bound.
No kernel may reach another device: no remote copies, remote signals or barrier semaphores. Data moves between devices by JAX's collectives and lax.ppermute only.
A program may use at most 64 MiB of HBM per device.

v0:
```python
import math

import jax
import jax.numpy as jnp
from jax import lax
from jax.sharding import PartitionSpec as P


def local(left, right, out_weight, out_bias, cotangent):
    left_complete = lax.all_gather(left, "narrow", axis=0, tiled=True)
    right_full = lax.all_gather(right, "wide", axis=0, tiled=True)
    alignment_rows = left_complete.shape[0]
    channel_count = left_complete.shape[1]
    tile_rows = left_complete.shape[2]
    tile_columns = right_full.shape[2]
    pair_width = cotangent.shape[2]
    rows_per_block = math.gcd(16, tile_rows)
    total_block_count = tile_rows // rows_per_block
    kept_rows = alignment_rows // lax.axis_size("narrow")

    def block_step(block_index, carry):
        running, pairs, grads = carry
        start = (block_index * rows_per_block).astype(jnp.int32)
        left_block = lax.dynamic_slice_in_dim(left_complete, start, rows_per_block, 2)
        cot_block = lax.dynamic_slice_in_dim(cotangent, start, rows_per_block, 0)
        outer_sum = (
            jnp.einsum("sci,sej->ijce", left_block, right_full, preferred_element_type=jnp.float32)
            / alignment_rows
        )
        outer_flat = outer_sum.astype(jnp.bfloat16).reshape(
            rows_per_block * tile_columns, channel_count * channel_count
        )
        pair_out = jnp.dot(outer_flat, out_weight, preferred_element_type=jnp.float32) + out_bias
        pair_out = pair_out.astype(jnp.bfloat16).reshape(rows_per_block, tile_columns, pair_width)
        cot_flat = cot_block.reshape(rows_per_block * tile_columns, pair_width)
        d_outer = lax.dot_general(
            cot_flat, out_weight, (((1,), (1,)), ((), ())), preferred_element_type=jnp.float32
        )
        d_outer = d_outer.astype(jnp.bfloat16).reshape(
            rows_per_block, tile_columns, channel_count, channel_count
        )
        grad_block = (
            jnp.einsum("ijce,sej->sci", d_outer, right_full, preferred_element_type=jnp.float32)
            / alignment_rows
        )
        running = (
            running
            + jnp.einsum("ijce,sci->sej", d_outer, left_block, preferred_element_type=jnp.float32)
            / alignment_rows
        )
        grad_block = lax.psum_scatter(grad_block, "narrow", scatter_dimension=0, tiled=True)
        pairs = lax.dynamic_update_slice_in_dim(pairs, pair_out, start, 0)
        grads = lax.dynamic_update_slice_in_dim(grads, grad_block, start, 2)
        return (running, pairs, grads)

    starting_value = (
        jnp.zeros((alignment_rows, channel_count, tile_columns), jnp.float32),
        jnp.zeros((tile_rows, tile_columns, pair_width), jnp.bfloat16),
        jnp.zeros((kept_rows, channel_count, tile_rows), jnp.float32),
    )
    right_terms, pair_update, grad_terms = lax.fori_loop(
        0, total_block_count, block_step, starting_value
    )
    grad_right = lax.psum_scatter(right_terms, "wide", scatter_dimension=0, tiled=True)
    return (pair_update, grad_terms, grad_right)


def solution(mesh):
    return jax.shard_map(
        local,
        mesh=mesh,
        in_specs=(
            P("narrow", None, "wide"),
            P("wide", None, "narrow"),
            P(),
            P(),
            P("wide", "narrow", None),
        ),
        out_specs=(P("wide", "narrow", None), P("narrow", None, "wide"), P("wide", None, "narrow")),
        check_vma=False,
    )
```

profile of v0, /device:TPU:0, one launch (start us, length us, event | category | flops | bytes accessed | tf_op | source)
XLA Modules:
  0.0 147.1 jit_solution(11280594527067747907)
XLA Ops:
  8.0 0.9 copy.29
  9.0 14.5 %all_gather.6 = bf16[32,32,32]{1,0,2:T(8,128)(2,1)S(1)} all-gather(bf16[8,32,32]{1,0,2:T(8,128)(2,1)S(1)} %copy.29), channel_id=1, replica_groups=mesh['wide'=8,'narrow'=4] {'narrow'}, dimensions={0}, use_global_device_ids=true | all-gather | bytes 81920 | tf_op jit(solution)/shard_map/all_gather | solution.py:10
  23.4 9.5 %all_gather.7 = bf16[32,32,64]{2,1,0:T(8,128)(2,1)S(1)} all-gather(bf16[4,32,64]{2,1,0:T(8,128)(2,1)} %param.8), channel_id=1, replica_groups=mesh['wide'=8,'narrow'=4] {'wide'}, dimensions={0}, use_global_device_ids=true | all-gather | bytes 147456 | tf_op jit(solution)/shard_map/all_gather | solution.py:11
  33.0 0.1 copy.30
  33.1 0.1 broadcast_in_dim.13
  33.2 70.0 %while.18 = (s32[]{:T(128)}, f32[32,32,64]{2,0,1:T(8,128)}, bf16[32,64,128]{2,1,0:T(8,128)(2,1)S(1)}, f32[8,32,32]{1,2,0:T(8,128)S(1)}, bf16[32,32,32]{1,0,2:T(8...) while((s32[]{:T(128)}, f32[32,32,64]{2,0,1:T(8,128)}, ...), condition=%wide.region_2.0_spmd.clone, body=%wide.region_0.0_spmd.clone.sunk | while | flops 741818368 | bytes 32361256 | solution.py:61
  33.2 0.0 reduce-scatter.5.cloned.1.call-start
  33.3 1.0 constant_dynamic-slice_fusion.2
  34.2 3.0 %convolution_convert_fusion.2 = bf16[1024,1024]{1,0:T(8,128)(2,1)} fusion(bf16[1024,128]{1,0:T(8,128)(2,1)S(1)} %bitcast.82, bf16[1024,128]{1,0:T(8,128)(2,1)} %get-tuple-element.315), kind=kOutput, calls=%fused_computation.4.clone.1 | convolution fusion | flops 269484032 | bytes 2621440 | tf_op jit(solution)/shard_map/while/body/eval_jaxpr/dot_general | solution.py:36
  37.2 2.9 %copy.53 = bf16[1024,1024]{0,1:T(8,128)(2,1)S(1)} copy(bf16[1024,1024]{1,0:T(8,128)(2,1)} %convolution_convert_fusion.2) | data formatting | bytes 4194304 | tf_op jit(solution)/shard_map/while/body/eval_jaxpr/convert_element_type | solution.py:39
  40.1 4.0 %reshape.46 = bf16[16,64,32,32]{1,0,3,2:T(8,128)(2,1)} reshape(bf16[1024,1024]{0,1:T(8,128)(2,1)S(1)} %copy.53) | data formatting | bytes 4194304 | tf_op jit(solution)/shard_map/while/body/eval_jaxpr/reshape | solution.py:39
  44.1 3.4 %fusion.58 = f32[32,32,16]{0,2,1:T(8,128)S(1)} fusion(bf16[16,64,32,32]{1,0,3,2:T(8,128)(2,1)} %reshape.46, bf16[32,32,64]{2,0,1:T(8,128)(2,1)S(1)} %get-tuple-element.316), kind=kOutput, calls=%fused_computation.13.clone.1 | convolution fusion | flops 67125248 | bytes 2293760 | tf_op jit(solution)/shard_map/while/body/eval_jaxpr/ijce,sej->sci/dot_general | solution.py:43
  47.5 0.9 copy.55
  48.4 0.0 reduce-scatter.5.cloned.1.call-update
  48.4 1.3 fusion.56
  49.7 4.7 %copy.54 = bf16[16,64,32,32]{1,0,3,2:T(8,128)(2,1)} copy(bf16[16,64,32,32]{1,2,3,0:T(8,128)(2,1)S(1)} %fusion.56) | data formatting | bytes 4194304 | tf_op jit(solution)/shard_map/while/body/eval_jaxpr/convert_element_type | solution.py:30
  54.4 5.5 %reshape.47 = bf16[1024,1024]{0,1:T(8,128)(2,1)S(1)} reshape(bf16[16,64,32,32]{1,0,3,2:T(8,128)(2,1)} %copy.54) | data formatting | bytes 4194304 | tf_op jit(solution)/shard_map/while/body/eval_jaxpr/reshape | solution.py:30
  59.8 0.0 copy-start
  59.8 0.0 copy-start.2
  59.9 5.7 %fusion.55 = f32[32,32,64]{2,0,1:T(8,128)} fusion(bf16[16,64,32,32]{1,0,3,2:T(8,128)(2,1)} %reshape.46, f32[32,32,64]{2,0,1:T(8,128)} %get-tuple-element.297, pred[]{:T(512)S(6)} %compare.3, bf16[32,32,32]{1,0,2:T(8,128)(2,1)S(1)} %get-tuple-element.313, s32[]{:T(128)S(6)} %select_n.12), kind=kOutput, calls=%fused_computation.9.clone.1 | convolution fusion | flops 67305472 | bytes 2752517 | tf_op jit(solution)/shard_map/while/body/eval_jaxpr/ijce,sci->sej/dot_general | solution.py:48
  65.5 0.0 copy-done
  65.5 0.7 fusion.57
  66.3 1.6 %reduce-scatter.5.cloned.1.call-done = f32[8,32,16]{1,2,0:T(8,128)} async-done(((f32[32,32,16]{1,2,0:T(8,128)}), f32[8,32,16]{1,2,0:T(8,128)}) %reduce-scatter.5.cloned.1.call-update) | async-done | bytes 16400 | tf_op jit(solution)/shard_map/while/body/eval_jaxpr/reduce_scatter | solution.py:51
  67.9 0.8 constant_dynamic-update-slice_fusion.5
  68.8 0.0 reduce-scatter.5.cloned.1.call-start
  68.8 1.0 constant_dynamic-slice_fusion.2
  69.8 3.0 %convolution_convert_fusion.2 = bf16[1024,1024]{1,0:T(8,128)(2,1)} fusion(bf16[1024,128]{1,0:T(8,128)(2,1)S(1)} %bitcast.82, bf16[1024,128]{1,0:T(8,128)(2,1)} %get-tuple-element.315), kind=kOutput, calls=%fused_computation.4.clone.1 | convolution fusion | flops 269484032 | bytes 2621440 | tf_op jit(solution)/shard_map/while/body/eval_jaxpr/dot_general | solution.py:36
  72.8 2.9 %copy.53 = bf16[1024,1024]{0,1:T(8,128)(2,1)S(1)} copy(bf16[1024,1024]{1,0:T(8,128)(2,1)} %convolution_convert_fusion.2) | data formatting | bytes 4194304 | tf_op jit(solution)/shard_map/while/body/eval_jaxpr/convert_element_type | solution.py:39
  75.6 4.0 %reshape.46 = bf16[16,64,32,32]{1,0,3,2:T(8,128)(2,1)} reshape(bf16[1024,1024]{0,1:T(8,128)(2,1)S(1)} %copy.53) | data formatting | bytes 4194304 | tf_op jit(solution)/shard_map/while/body/eval_jaxpr/reshape | solution.py:39
  79.6 3.4 %fusion.58 = f32[32,32,16]{0,2,1:T(8,128)S(1)} fusion(bf16[16,64,32,32]{1,0,3,2:T(8,128)(2,1)} %reshape.46, bf16[32,32,64]{2,0,1:T(8,128)(2,1)S(1)} %get-tuple-element.316), kind=kOutput, calls=%fused_computation.13.clone.1 | convolution fusion | flops 67125248 | bytes 2293760 | tf_op jit(solution)/shard_map/while/body/eval_jaxpr/ijce,sej->sci/dot_general | solution.py:43
  83.0 0.9 copy.55
  83.9 0.0 reduce-scatter.5.cloned.1.call-update
  83.9 1.3 fusion.56
  85.2 4.7 %copy.54 = bf16[16,64,32,32]{1,0,3,2:T(8,128)(2,1)} copy(bf16[16,64,32,32]{1,2,3,0:T(8,128)(2,1)S(1)} %fusion.56) | data formatting | bytes 4194304 | tf_op jit(solution)/shard_map/while/body/eval_jaxpr/convert_element_type | solution.py:30
  89.9 5.5 %reshape.47 = bf16[1024,1024]{0,1:T(8,128)(2,1)S(1)} reshape(bf16[16,64,32,32]{1,0,3,2:T(8,128)(2,1)} %copy.54) | data formatting | bytes 4194304 | tf_op jit(solution)/shard_map/while/body/eval_jaxpr/reshape | solution.py:30
  95.4 0.0 copy-start
  95.4 0.0 copy-start.2
  95.4 5.8 %fusion.55 = f32[32,32,64]{2,0,1:T(8,128)} fusion(bf16[16,64,32,32]{1,0,3,2:T(8,128)(2,1)} %reshape.46, f32[32,32,64]{2,0,1:T(8,128)} %get-tuple-element.297, pred[]{:T(512)S(6)} %compare.3, bf16[32,32,32]{1,0,2:T(8,128)(2,1)S(1)} %get-tuple-element.313, s32[]{:T(128)S(6)} %select_n.12), kind=kOutput, calls=%fused_computation.9.clone.1 | convolution fusion | flops 67305472 | bytes 2752517 | tf_op jit(solution)/shard_map/while/body/eval_jaxpr/ijce,sci->sej/dot_general | solution.py:48
  101.2 0.0 copy-done
  101.2 0.7 fusion.57
  102.0 0.4 reduce-scatter.5.cloned.1.call-done
  102.4 0.8 constant_dynamic-update-slice_fusion.5
  103.2 0.0 reduce-scatter.3.cloned.1.call-start
  103.2 2.3 %copy.31 = f32[32,32,64]{2,1,0:T(8,128)} copy(f32[32,32,64]{2,0,1:T(8,128)} %get-tuple-element.161) | data formatting | bytes 524288 | tf_op jit(solution)/shard_map/while | solution.py:61
  105.6 0.0 reduce-scatter.3.cloned.1.call-update
  105.6 0.8 copy.32
  106.3 33.4 %reduce-scatter.3.cloned.1.call-done = f32[4,32,64]{2,1,0:T(8,128)} async-done(((f32[32,32,64]{2,1,0:T(8,128)}), f32[4,32,64]{2,1,0:T(8,128)}) %reduce-scatter.3.cloned.1.call-update) | async-done | bytes 32784 | tf_op jit(solution)/shard_map/reduce_scatter | solution.py:64
  139.7 0.0 copy-done.1
  (7 shorter events, 0.1 us)
Async XLA Ops:
  33.2 34.7 %reduce-scatter.5.cloned.1.call-start = ((), (), s32[]{:S(2)}) async-start(), calls=%async_computation.3 | async-start | bytes 327680 | tf_op jit(solution)/shard_map/while/body/eval_jaxpr/reduce_scatter | solution.py:51
  59.8 5.7 %copy-start = (bf16[1024,128]{1,0:T(8,128)(2,1)S(1)}, bf16[1024,128]{1,0:T(8,128)(2,1)}, u32[]{:S(2)}) copy-start(bf16[1024,128]{1,0:T(8,128)(2,1)} %get-tuple-element.315) | copy-start | bytes 786436 | tf_op jit(solution)/shard_map/while
  59.8 5.7 %copy-start.2 = (f32[128]{0:T(128)S(1)}, f32[128]{0:T(128)}, u32[]{:S(2)}) copy-start(f32[128]{0:T(128)} %get-tuple-element.317) | copy-start | bytes 1540 | tf_op jit(solution)/shard_map/while
  68.8 33.6 %reduce-scatter.5.cloned.1.call-start = ((), (), s32[]{:S(2)}) async-start(), calls=%async_computation.3 | async-start | bytes 327680 | tf_op jit(solution)/shard_map/while/body/eval_jaxpr/reduce_scatter | solution.py:51
  95.4 5.8 %copy-start = (bf16[1024,128]{1,0:T(8,128)(2,1)S(1)}, bf16[1024,128]{1,0:T(8,128)(2,1)}, u32[]{:S(2)}) copy-start(bf16[1024,128]{1,0:T(8,128)(2,1)} %get-tuple-element.315) | copy-start | bytes 786436 | tf_op jit(solution)/shard_map/while
  95.4 5.8 %copy-start.2 = (f32[128]{0:T(128)S(1)}, f32[128]{0:T(128)}, u32[]{:S(2)}) copy-start(f32[128]{0:T(128)} %get-tuple-element.317) | copy-start | bytes 1540 | tf_op jit(solution)/shard_map/while
  103.2 36.5 %copy-start.1 = (bf16[32,64,128]{2,1,0:T(8,128)(2,1)}, bf16[32,64,128]{2,1,0:T(8,128)(2,1)S(1)}, u32[]{:S(2)}) copy-start(bf16[32,64,128]{2,1,0:T(8,128)(2,1)S(1)} %get-tuple-element.207) | copy-start | bytes 1572868
  103.2 36.5 %reduce-scatter.3.cloned.1.call-start = ((), (), s32[]{:S(2)}) async-start(), calls=%async_computation.2 | async-start | bytes 589824 | tf_op jit(solution)/shard_map/reduce_scatter | solution.py:64
Sparse Core Ops, SparseCore 0:
  48.5 19.3 reduce-scatter.4
  84.0 18.2 reduce-scatter.4
Sparse Core Ops, SparseCore 1:
  107.3 32.3 reduce-scatter.2
where the time goes:
time: 148 us; the launch traced here: 147 us
  local copies, waits for them, and re-layouts  43.7 us (30%)
  waiting for transfers between devices  35.4 us (24%)
  matrix products  28.3 us (19%)
  blocking collectives  24 us (16%)
  between operations  15.5 us (10%)
    reduce_scatter x1, waiting for transfers between devices, local(): lax.psum_scatter(right_terms, 'wide', scatter_dimension=0, tiled=True)  33.4 us
    all_gather x1, blocking collectives, local(): left_complete = lax.all_gather(left, 'narrow', axis=0, tiled=True)  14.5 us
    dot_general x2, matrix products, block_step(): jnp.einsum('ijce,sci->sej', d_outer, left_block, preferred_element_type=j...  11.5 us
    reshape x2, local copies, waits for them, and re-layouts, block_step(): outer_sum.astype(jnp.bfloat16)  10.9 us
    all_gather x1, blocking collectives, local(): right_full = lax.all_gather(right, 'wide', axis=0, tiled=True)  9.51 us
    convert_element_type x2, local copies, waits for them, and re-layouts, block_step(): outer_sum.astype(jnp.bfloat16)  9.33 us
    reshape x2, local copies, waits for them, and re-layouts, block_step(): d_outer.astype(jnp.bfloat16)  7.98 us
    dot_general x2, matrix products, block_step(): jnp.einsum('ijce,sej->sci', d_outer, right_full, preferred_element_type=j...  6.81 us
  transfers between devices with their start and end apart: 3, of which 3 were waited for; matrix products, arithmetic and copies ran while one was open for 25% of the time, Pallas kernels for 0%

commit v1 on v0

v1 whole, which is shorter than its diff:
```python
import functools

import jax
import jax.numpy as jnp
from jax import lax
from jax.experimental import pallas as pl
from jax.experimental.pallas import tpu as pltpu
from jax.sharding import PartitionSpec as P


LANES = 128
MXU = 256
NT = (((1,), (1,)), ((), ()))
NN = (((1,), (0,)), ((), ()))


def dot(a, b, dims):
    return lax.dot_general(a, b, dims, preferred_element_type=jnp.float32)


def loop(count, body, small):
    if small:
        for n in range(count):
            body(n)
    else:
        lax.fori_loop(0, count, lambda n, c: (body(n), c)[1], 0)


def block_transpose(tile):
    size, lanes = tile.shape
    width = lanes // size
    row = lax.broadcasted_iota(jnp.int32, tile.shape, 0)
    block = lax.broadcasted_iota(jnp.int32, tile.shape, 1) // width
    result = tile
    for d in range(1, size):
        moved = pltpu.roll(pltpu.roll(tile, size - d, 0), width * d, 1)
        result = jnp.where(block == (row + d) % size, moved, result)
    return result


def block_diagonal(right_f32, first, rows, channels, columns, copies):
    pack = LANES // columns
    here = right_f32[pl.ds(first, rows, stride=channels // pack), :]
    lane = lax.broadcasted_iota(jnp.int32, here.shape, 1) // columns
    zero = jnp.zeros_like(here)
    moved = [here] + [pltpu.roll(here, n * columns, 1) for n in range(1, pack)]
    found = []
    for h in range(pack):
        blocks = []
        for n in range(copies):
            part = jnp.where(lane == n % pack, moved[(n - h) % pack], zero)
            tiles = [part if t == n // pack else zero for t in range(copies // pack)]
            blocks.append(jnp.concatenate(tiles, axis=1))
        found.append(jnp.concatenate(blocks, axis=0).astype(jnp.bfloat16))
    return found


def place_right(right_refs, right_f32):
    place = lax.axis_index("wide")
    for ref, keys in right_refs:
        rows = ref.shape[1]
        for n, key in enumerate(keys):
            start = pl.multiple_of((place ^ key) * rows, rows)
            right_f32[pl.ds(start, rows), :] = ref[n].astype(jnp.float32)


def place_left(left_refs, left_f32):
    place = lax.axis_index("narrow")
    for ref, keys in left_refs:
        for n, key in enumerate(keys):
            for copy in range(ref.shape[1]):
                left_f32[copy, place ^ key] = ref[n, copy].astype(jnp.float32)
    copies, places, part, lanes = left_f32.shape
    return left_f32[...].reshape(copies * places * part, lanes)


def dense(ref, out):
    rows, channels, columns = ref.shape
    pack = LANES // columns
    half = channels // pack
    for s in range(rows):
        block = ref[s].astype(jnp.float32)
        block = [block[h * half : (h + 1) * half] for h in range(pack)]
        out[s * half : (s + 1) * half, :] = jnp.concatenate(block, axis=1).astype(out.dtype)


def prepare_kernel(inside, *refs):
    sources, (left_out, *outs), (left_ref, sent) = refs[:4], refs[4:8], refs[8:]
    moves = [
        pltpu.make_async_copy(source, target, sent.at[n])
        for n, (source, target) in enumerate(zip(sources, [left_ref] + outs))
    ]
    for move in moves:
        move.start()
    moves[0].wait()
    if inside:
        part, channels, tile_rows = left_ref.shape
        flat = left_ref[...].astype(jnp.float32).reshape(part * channels, tile_rows).T
        for n in range(left_out.shape[1]):
            piece = block_transpose(flat[n * part : (n + 1) * part])
            left_out[0, n] = piece.astype(left_out.dtype)
    else:
        left_out[0] = left_ref[...]
    for move in moves[1:]:
        move.wait()


def weight_kernel(weight_ref, by_e_ref, transposed_ref, weight_f32):
    channels = by_e_ref.shape[0]
    weight_f32[...] = weight_ref[...].astype(jnp.float32)
    for e in range(channels):
        by_e_ref[e] = weight_f32[pl.ds(e, channels, stride=channels), :].astype(jnp.bfloat16)
    flat = by_e_ref[...].reshape(channels * channels, weight_ref.shape[1])
    transposed_ref[...] = flat.astype(jnp.float32).T.astype(jnp.bfloat16)


def stack_kernel(raw, one, other, *refs):
    out = refs[-1]
    count = out.shape[0] // 2
    if raw:
        dense(one, out.at[0])
        dense(other, out.at[1])
    else:
        out[:count] = one[...]
        out[count:] = other[...]


def d_outer_kernel(sizes, first, cot_ref, weight_ref, d_ref):
    _, channels, copies, groups, _ = sizes
    count = d_ref.shape[1] // channels
    per_dot = min(channels, MXU // channels)

    def step(g):
        slab = [cot_ref[n * groups + first + g] for n in range(copies)]
        slab = jnp.concatenate(slab, axis=0)
        for start in range(0, channels, per_dot):
            weight = weight_ref[start : start + per_dot].reshape(per_dot * channels, -1)
            piece = dot(weight, slab, NT).astype(jnp.bfloat16)
            for e in range(per_dot):
                at = pl.ds(g * channels, channels)
                d_ref[start + e, at, :] = piece[e * channels : (e + 1) * channels]

    loop(count, step, count <= 8)


def gradient_kernel(sizes, left_keys, right_keys, *refs):
    rows, channels, copies, _, columns = sizes
    n_left, n_right = len(left_keys), len(right_keys)
    left_refs, refs = list(zip(refs[:n_left], left_keys)), refs[n_left:]
    right_refs, refs = list(zip(refs[:n_right], right_keys)), refs[n_right:]
    d_refs, refs = refs[:-8], refs[-8:]
    left_kept, left_sent, right_kept, right_sent, left_f32, right_f32, left_sum, right_sum = refs
    place_right(right_refs, right_f32)
    left_mat = place_left(left_refs, left_f32).astype(jnp.bfloat16)
    pack = LANES // columns
    scale = 1.0 / rows
    half = channels // pack
    low = lax.broadcasted_iota(jnp.int32, (rows, LANES), 1) < columns
    small = left_mat.shape[1] <= MXU

    def diagonal(outer):
        found = []
        for h in range(pack):
            total = None
            for t in range(copies // pack):
                n = t * pack + h
                piece = outer[n * rows : (n + 1) * rows, t * LANES : (t + 1) * LANES]
                total = piece if total is None else total + piece
            found.append(total)
        return found

    if not small:
        left_sum[...] = jnp.zeros_like(left_sum)
    totals = []

    def step(first):
        found = []
        diag = block_diagonal(right_f32, first, rows, channels, columns, copies)
        for h in range(pack):
            e = first + h * half
            d_e = jnp.concatenate([ref[e] for ref in d_refs], axis=0)
            term = dot(d_e, diag[h], NT)
            if small:
                totals.append(term)
            else:
                left_sum[...] += term
            found.append(diagonal(dot(left_mat, d_e, NN)))
        if pack == 1:
            result = found[0][0]
        else:
            straight = jnp.where(low, found[0][0], found[1][1])
            crossed = jnp.where(low, found[1][0], found[0][1])
            result = straight + pltpu.roll(crossed, columns, 1)
        right_sum[pl.ds(first, rows, stride=half), :] = result * scale

    loop(half, step, small)
    if small:
        total = totals[0]
        for term in totals[1:]:
            total = total + term
        left_sum[...] = total

    place = lax.axis_index("wide")
    for n in range(right_kept.shape[0]):
        count = right_kept.shape[1]
        for key, ref in ((2 * n, right_kept), (2 * n + 1, right_sent)):
            start = pl.multiple_of((place ^ key) * count, count)
            ref[n] = right_sum[pl.ds(start, count), :].astype(ref.dtype)
    left_f32[...] = (left_sum[...].T * scale).reshape(left_f32.shape)
    place = lax.axis_index("narrow")
    for n in range(left_kept.shape[0]):
        for key, ref in ((2 * n, left_kept), (2 * n + 1, left_sent)):
            for copy in range(copies):
                ref[n, copy] = left_f32[copy, place ^ key].astype(ref.dtype)


def forward_kernel(sizes, left_keys, right_keys, first, aliased, *refs):
    rows, channels, copies, groups, columns = sizes
    n_left, n_right = len(left_keys), len(right_keys)
    weight_ref, bias_ref, refs = refs[0], refs[1], refs[2:]
    left_refs, refs = list(zip(refs[:n_left], left_keys)), refs[n_left:]
    right_refs, refs = list(zip(refs[:n_right], right_keys)), refs[n_right:]
    out_ref, left_f32, right_f32, outer_t, pairs, sent = refs[1:] if aliased else refs
    count = outer_t.shape[0]
    place_right(right_refs, right_f32)
    left_t = place_left(left_refs, left_f32).T.astype(jnp.bfloat16)
    left_t = left_t[first * channels : (first + count) * channels]
    pack = LANES // columns
    half = channels // pack
    scale = 1.0 / rows
    bias = bias_ref[...]
    small = count <= 8

    def e_step(start):
        diag = block_diagonal(right_f32, start, rows, channels, columns, copies)
        for h in range(pack):
            outer = (dot(left_t, diag[h], NN) * scale).astype(jnp.bfloat16)
            at = pl.ds((start + h * half) * channels, channels)
            for g in range(count):
                outer_t[g, at, :] = outer[g * channels : (g + 1) * channels]

    loop(half, e_step, small)

    def g_step(g):
        pair = dot(weight_ref[...], outer_t[g], NN).T + bias
        pair = pair.astype(jnp.bfloat16)
        for n in range(copies):
            pairs[n * count + g] = pair[n * columns : (n + 1) * columns]

    loop(count, g_step, small)
    moves = []
    for n in range(copies):
        source = pairs.at[pl.ds(n * count, count)]
        target = out_ref.at[pl.ds(n * groups + first, count)]
        moves.append(pltpu.make_async_copy(source, target, sent.at[n]))
        moves[-1].start()
    for move in moves:
        move.wait()


def add_kernel(*refs):
    (left_kept, left_new, right_kept, right_new), outs = refs[:4], refs[4:]
    for n in range(left_kept.shape[0]):
        total = left_kept[n] + left_new[n].astype(jnp.float32)
        outs[n][...] = total.astype(outs[n].dtype)
    outs = outs[left_kept.shape[0] :]
    for n in range(right_kept.shape[0]):
        total = right_kept[n] + right_new[n].astype(jnp.float32)
        outs[n][...] = total.astype(outs[n].dtype)


def sum_kernel(n_left, inside, *refs):
    left_refs, refs = refs[:n_left], refs[n_left:]
    right_refs, (left_out, right_out) = refs[:-2], refs[-2:]
    total = left_refs[0][...]
    for ref in left_refs[1:]:
        total = total + ref[...].astype(jnp.float32)
    if inside:
        total = jnp.concatenate([block_transpose(total[n]) for n in range(total.shape[0])], axis=0)
        left_out[...] = total.T.reshape(left_out.shape)
    else:
        left_out[...] = total
    total = right_refs[0][...]
    for ref in right_refs[1:]:
        total = total + ref[...].astype(jnp.float32)
    rows, channels, columns = right_out.shape
    pack = LANES // columns
    half = channels // pack
    for s in range(rows):
        part = total[s * half : (s + 1) * half]
        for h in range(pack):
            right_out[s, h * half : (h + 1) * half, :] = part[:, h * columns : (h + 1) * columns]


def exchange(x, axis, m):
    size = lax.axis_size(axis)
    return lax.ppermute(x, axis, [(n, n ^ m) for n in range(size)])


def powers(size):
    return [1 << n for n in range(size.bit_length() - 1)]


def vmem(count):
    return [pl.BlockSpec(memory_space=pltpu.VMEM)] * count


def tile(left, right, out_weight, out_bias, cotangent):
    n_narrow, n_wide = lax.axis_size("narrow"), lax.axis_size("wide")
    part, channels, tile_rows = left.shape
    right_part, _, columns = right.shape
    width = cotangent.shape[2]
    rows = part * n_narrow
    copies = MXU // columns
    groups = tile_rows // copies
    pack = LANES // columns
    inside = part == groups and channels * part == MXU
    halves = 2
    count = groups // halves
    sizes = (rows, channels, copies, groups, columns)
    f32, bf16 = jnp.float32, jnp.bfloat16
    shape = jax.ShapeDtypeStruct
    work = channels * channels * tile_rows * columns
    limit = min(56 << 20, max(12 << 20, 3 * work))
    flops = 2 * work * width
    anywhere = pl.BlockSpec(memory_space=pl.ANY)
    outside = pl.BlockSpec(memory_space=pltpu.HBM)

    def call(kernel, outs, args, scratch=(), cost=0, in_specs=None, out_specs=None, **more):
        return pl.pallas_call(
            kernel,
            in_specs=in_specs or vmem(len(args)),
            out_specs=out_specs or vmem(len(outs)),
            out_shape=outs,
            scratch_shapes=scratch,
            compiler_params=pltpu.CompilerParams(vmem_limit_bytes=limit),
            cost_estimate=pl.CostEstimate(flops=cost, bytes_accessed=1 << 16, transcendentals=0),
            **more,
        )(*args)

    left_shape = (copies, part, groups * channels)
    right_shape = (right_part * channels // pack, LANES)

    hbm = functools.partial(pltpu.with_memory_space_constraint, memory_space=pltpu.HBM)

    steps = powers(n_wide)[1:] + [1]
    right_new = exchange(right, "wide", steps[0])
    source = left
    if not inside:
        source = left.reshape(part, channels, copies, groups).transpose(2, 0, 3, 1)
        source = source.reshape(left_shape)
    sources = [source, right, out_weight, cotangent]
    lefts, rights, weight, cot = call(
        functools.partial(prepare_kernel, inside),
        [shape((1,) + left_shape, bf16)] + [shape(v.shape, bf16) for v in sources[1:]],
        [hbm(v) for v in sources],
        [pltpu.VMEM(source.shape, bf16), pltpu.SemaphoreType.DMA((4,))],
        cost=flops // 16,
        in_specs=[outside] * 4,
    )
    by_e, transposed = call(
        weight_kernel,
        [shape((channels, channels, width), bf16), shape((width, channels * channels), bf16)],
        [weight],
        [pltpu.VMEM(weight.shape, f32)],
        cost=flops // 8,
    )

    def stack(one, other, raw, after=()):
        shapes = right_shape if raw else one.shape[1:]
        outs = [shape((2 if raw else 2 * one.shape[0],) + shapes, bf16)]
        args = [one, other, *after]
        specs = vmem(2) + [anywhere] * len(after)
        return call(functools.partial(stack_kernel, raw), outs, args, in_specs=specs)[0]

    d_shape = shape((channels, count * channels, copies * columns), bf16)
    d_outer = []
    for n in range(halves):
        kernel = functools.partial(d_outer_kernel, sizes, n * count)
        d_outer += call(kernel, [d_shape], [cot, by_e], cost=flops // halves)

    keys = [0]
    for n, m in enumerate(steps):
        if n:
            right_new = exchange(rights, "wide", m)
        new = [k ^ m for k in keys]
        if n + 1 < len(steps):
            rights = stack(rights, right_new, n == 0, d_outer[n : n + 1])
            keys = keys + new
    right_keys, rights = (keys, new), [rights, right_new]

    keys = [0]
    steps = powers(n_narrow)[::-1]
    for n, m in enumerate(steps):
        left_new = exchange(lefts, "narrow", m)
        new = [k ^ m for k in keys]
        if n + 1 < len(steps):
            lefts = stack(lefts, left_new, False, d_outer[1:2] if n == 0 else ())
            keys = keys + new
    left_keys, lefts = (keys, new), [lefts, left_new]

    left_f32 = pltpu.VMEM((copies, n_narrow, part, groups * channels), f32)
    right_f32 = pltpu.VMEM((rows * channels // pack, LANES), f32)
    far, near = n_narrow // 2, n_wide // 2
    left_kept, left_sent, right_kept, right_sent = call(
        functools.partial(gradient_kernel, sizes, left_keys, right_keys),
        [
            shape((far,) + left_shape, f32),
            shape((far,) + left_shape, bf16),
            shape((near,) + right_shape, f32),
            shape((near,) + right_shape, bf16),
        ],
        [*lefts, *rights, *d_outer],
        [
            left_f32,
            right_f32,
            pltpu.VMEM((groups * channels, copies * rows), f32),
            pltpu.VMEM((rows * channels // pack, LANES), f32),
        ],
        cost=flops * 2,
    )
    left_new = exchange(left_sent, "narrow", 1)
    right_new = exchange(right_sent, "wide", 1)

    def forward(first, before):
        args = [transposed, out_bias.reshape(1, width), *lefts, *rights]
        specs, more = vmem(len(args)), {}
        if before is not None:
            more = {"input_output_aliases": {len(args): 0}}
            args, specs = args + [before], specs + [anywhere]
        return call(
            functools.partial(
                forward_kernel, sizes, left_keys, right_keys, first, before is not None
            ),
            [shape(cotangent.shape, bf16)],
            args,
            [
                left_f32,
                right_f32,
                pltpu.VMEM((count, channels * channels, copies * columns), bf16),
                pltpu.VMEM((copies * count, columns, width), bf16),
                pltpu.SemaphoreType.DMA((copies,)),
            ],
            cost=flops,
            in_specs=specs,
            out_specs=[anywhere],
            **more,
        )[0]

    pair_update = forward(0, None)
    sums = call(
        add_kernel,
        [shape(left_shape, bf16 if n else f32) for n in range(far)]
        + [shape(right_shape, bf16 if n else f32) for n in range(near)],
        [left_kept, left_new, right_kept, right_new],
    )
    left_sums = [exchange(v, "narrow", 2 * n) if n else v for n, v in enumerate(sums[:far])]
    right_sums = [exchange(v, "wide", 2 * n) if n else v for n, v in enumerate(sums[far:])]
    for n in range(1, halves):
        pair_update = forward(n * count, pair_update)

    grad_left, grad_right = call(
        functools.partial(sum_kernel, far, inside),
        [
            shape((part, channels, tile_rows) if inside else left_shape, f32),
            shape((right_part, channels, columns), f32),
        ],
        [*left_sums, *right_sums],
    )
    if not inside:
        grad_left = grad_left.reshape(copies, part, groups, channels).transpose(1, 3, 0, 2)
        grad_left = grad_left.reshape(part, channels, tile_rows)
    return pair_update, grad_left, grad_right


def solution(mesh):
    return jax.shard_map(
        tile,
        mesh=mesh,
        in_specs=(
            P("narrow", None, "wide"),
            P("wide", None, "narrow"),
            P(),
            P(),
            P("wide", "narrow", None),
        ),
        out_specs=(P("wide", "narrow", None), P("narrow", None, "wide"), P("wide", None, "narrow")),
        check_vma=False,
    )
```

time: 148 us -> 35.5 us (0.24)
  local copies, waits for them, and re-layouts: 43.7 us -> 0.01 us
  waiting for transfers between devices: 35.4 us -> 6.5 us
  matrix products: 28.3 us -> 0 us
  blocking collectives: 24 us -> 0 us
  starting transfers between devices: 0.08 us -> 18.1 us
  between operations: 15.5 us -> 0.74 us
  Pallas kernels: 0 us -> 10 us
    reduce_scatter x3 -> x0, waiting for transfers between devices: 35.3 us -> none  [the longest x1 33.4 us: local(): lax.psum_scatter(right_terms, 'wide', scatter_dimension=0, tiled=True)]
    dot_general x10 -> x0, matrix products: 28.3 us -> none  [the longest x2 11.5 us: block_step(): jnp.einsum('ijce,sci->sej', d_outer, left_block, preferred_element_type=j...]
    all_gather x2 -> x0, blocking collectives: 24 us -> none  [the longest x1 14.5 us: local(): left_complete = lax.all_gather(left, 'narrow', axis=0, tiled=True)]
    reshape x4 -> x0, local copies, waits for them, and re-layouts: 18.9 us -> none  [the longest x2 10.9 us: block_step(): outer_sum.astype(jnp.bfloat16)]
    ppermute x0 -> x11, starting transfers between devices: none -> 18.1 us  [exchange(): return lax.ppermute(x, axis, [(n, n ^ m) for n in range(size)])]
    convert_element_type x4 -> x0, local copies, waits for them, and re-layouts: 15 us -> none  [the longest x2 9.33 us: block_step(): outer_sum.astype(jnp.bfloat16)]
    pallas_call x0 -> x12, Pallas kernels: none -> 10 us  [call(): pl.pallas_call(kernel, in_specs=in_specs or vmem(len(args)), out_specs=ou...]
    ppermute x0 -> x11, waiting for transfers between devices: none -> 6.5 us  [exchange(): return lax.ppermute(x, axis, [(n, n ^ m) for n in range(size)])]
  transfers between devices with their start and end apart: 3 -> 11, of which waited for: 3 -> 6; matrix products, arithmetic and copies ran while one was open for 25% -> 0% of each run, Pallas kernels for 0% -> 20%
where the time goes in v1:
time: 35.5 us; the launch traced here: 35.4 us
  starting transfers between devices  18.1 us (51%)
  Pallas kernels  10 us (28%)
  waiting for transfers between devices  6.5 us (18%)
  between operations  0.74 us (2%)
    ppermute x11, starting transfers between devices, exchange(): return lax.ppermute(x, axis, [(n, n ^ m) for n in range(size)])  18.1 us
    pallas_call x12, Pallas kernels, call(): pl.pallas_call(kernel, in_specs=in_specs or vmem(len(args)), out_specs=ou...  10 us
    ppermute x11, waiting for transfers between devices, exchange(): return lax.ppermute(x, axis, [(n, n ^ m) for n in range(size)])  6.5 us
  transfers between devices with their start and end apart: 11, of which 6 were waited for; matrix products, arithmetic and copies ran while one was open for 0% of the time, Pallas kernels for 20%

profile of v1, /device:TPU:0, one launch (start us, length us, event | category | flops | bytes accessed | tf_op | source)
XLA Modules:
  0.0 35.4 jit_solution(5055045304385784089)
XLA Ops:
  0.6 3.0 %collective-permute-start.2 = (bf16[4,32,64]{2,1,0:T(8,128)(2,1)}, bf16[4,32,64]{2,1,0:T(8,128)(2,1)S(1)}, u32[]{:S(2)}, u32[]{:S(2)}) collective-permute-start(bf16[4,32,64]{2,1,0:T(8,128)(2,1)} %refs_1_.1), channel_id=1, source_target_pairs={{0,8},{4,12},{8,0},{12,4},{16,24},{20,28},{24,16},{28,20},{1,9},{5... | collective-permute-start | bytes 49160 | tf_op jit(solution)/shard_map/ppermute | solution.py:297
  3.7 1.2 %shard_map.76 = (bf16[1,4,8,256]{3,2,1,0:T(8,128)(2,1)S(1)}, bf16[4,32,64]{2,1,0:T(8,128)(2,1)S(1)}, bf16[1024,128]{1,0:T(8,128)(2,1)S(1)}, bf16[32,64,128]{2,1,0:T(8,128)(2,1)S(1)}) custom-call(bf16[8,32,32]{2,1,0:T(8,128)(2,1)} %refs_0_.1, bf16[4,32,64]{2,1,0:T(8,128)(2,1)} %refs_1_.1, bf16[1024,128]{1,0:T(8,128)(2,1)} %refs_2_.1, bf16[32,64,128]{2,1,0:T(8,128)(2,1)} %refs_3_.1), custom_call_target="tpu_custom_call" | custom-call | flops 33554432 | bytes 65536 | tf_op jit(solution)/shard_map/pallas_call | solution.py:330
  4.9 0.4 %shard_map.77 = (bf16[32,32,128]{2,1,0:T(8,128)(2,1)S(1)}, bf16[128,1024]{1,0:T(8,128)(2,1)S(1)}) custom-call(bf16[1024,128]{1,0:T(8,128)(2,1)S(1)} %get-tuple-element.21.weight_ref), custom_call_target="tpu_custom_call" | custom-call | flops 67108864 | bytes 65536 | tf_op jit(solution)/shard_map/pallas_call | solution.py:330
  5.3 0.7 %shard_map.80.refs_0_.refs_4_ = bf16[32,128,256]{2,1,0:T(8,128)(2,1)S(1)} custom-call(bf16[32,64,128]{2,1,0:T(8,128)(2,1)S(1)} %get-tuple-element.24.cot_ref, bf16[32,32,128]{2,1,0:T(8,128)(2,1)S(1)} %get-tuple-element.25.weight_ref), custom_call_target="tpu_custom_call" | custom-call | flops 268435456 | bytes 65536 | tf_op jit(solution)/shard_map/pallas_call | solution.py:330
  6.0 0.0 collective-permute-done.2.other
  6.0 0.1 shard_map.81.one
  6.1 1.9 %collective-permute-start.3 = (bf16[2,64,128]{2,1,0:T(8,128)(2,1)S(1)}, bf16[2,64,128]{2,1,0:T(8,128)(2,1)S(1)}, u32[]{:S(2)}, u32[]{:S(2)}) collective-permute-start(bf16[2,64,128]{2,1,0:T(8,128)(2,1)S(1)} %shard_map.81.one), channel_id=1, source_target_pairs={{0,16},{4,20},{8,24},{12,28},{16,0},{20,4},{24,8},{28,12},{1,17},{... | collective-permute-start | bytes 98312 | tf_op jit(solution)/shard_map/ppermute | solution.py:297
  8.0 0.7 %shard_map.78.refs_0_.refs_5_ = bf16[32,128,256]{2,1,0:T(8,128)(2,1)S(1)} custom-call(bf16[32,64,128]{2,1,0:T(8,128)(2,1)S(1)} %get-tuple-element.24.cot_ref, bf16[32,32,128]{2,1,0:T(8,128)(2,1)S(1)} %get-tuple-element.25.weight_ref), custom_call_target="tpu_custom_call" | custom-call | flops 268435456 | bytes 65536 | tf_op jit(solution)/shard_map/pallas_call | solution.py:330
  8.7 1.4 %collective-permute-done.3.other = bf16[2,64,128]{2,1,0:T(8,128)(2,1)S(1)} collective-permute-done((bf16[2,64,128]{2,1,0:T(8,128)(2,1)S(1)}, bf16[2,64,128]{2,1,0:T(8,128)(2,1)S(1)}, u32[]{:S(2)}, u32[]{:S(2)}) %collective-permute-start.3) | collective-permute-done | bytes 32800 | tf_op jit(solution)/shard_map/ppermute | solution.py:297
  10.1 0.0 collective-permute-start.4
  10.1 2.9 %collective-permute-start = (bf16[1,4,8,256]{3,2,1,0:T(8,128)(2,1)S(1)}, bf16[1,4,8,256]{3,2,1,0:T(8,128)(2,1)S(1)}, u32[]{:S(2)}, u32[]{:S(2)}) collective-permute-start(bf16[1,4,8,256]{3,2,1,0:T(8,128)(2,1)S(1)} %get-tuple-element.23.one), channel_id=1, source_target_pairs={{0,2},{1,3},{2,0},{3,1},{4,6},{5,7},{6,4},{7,5},{8,10},{9,11},{10,... | collective-permute-start | bytes 49160 | tf_op jit(solution)/shard_map/ppermute | solution.py:297
  13.0 1.8 %collective-permute-done.other = bf16[1,4,8,256]{3,2,1,0:T(8,128)(2,1)S(1)} collective-permute-done((bf16[1,4,8,256]{3,2,1,0:T(8,128)(2,1)S(1)}, bf16[1,4,8,256]{3,2,1,0:T(8,128)(2,1)S(1)}, u32[]{:S(2)}, u32[]{:S(2)}) %collective-permute-start) | collective-permute-done | bytes 16416 | tf_op jit(solution)/shard_map/ppermute | solution.py:297
  14.8 0.0 copy-start
  14.8 1.9 %collective-permute-start.1 = (bf16[2,4,8,256]{3,2,1,0:T(8,128)(2,1)S(1)}, bf16[2,4,8,256]{3,2,1,0:T(8,128)(2,1)S(1)}, u32[]{:S(2)}, u32[]{:S(2)}) collective-permute-start(bf16[2,4,8,256]{3,2,1,0:T(8,128)(2,1)S(1)} %shard_map.79.refs_2_.refs_0_), channel_id=1, source_target_pairs={{0,1},{1,0},{2,3},{3,2},{4,5},{5,4},{6,7},{7,6},{8,9},{9,8},{10,11... | collective-permute-start | bytes 98312 | tf_op jit(solution)/shard_map/ppermute | solution.py:297
  16.7 2.1 %collective-permute-done.1.refs_3_.refs_1_ = bf16[2,4,8,256]{3,2,1,0:T(8,128)(2,1)S(1)} collective-permute-done((bf16[2,4,8,256]{3,2,1,0:T(8,128)(2,1)S(1)}, bf16[2,4,8,256]{3,2,1,0:T(8,128)(2,1)S(1)}, u32[]{:S(2)}, u32[]{:S(2)}) %collective-permute-start.1) | collective-permute-done | bytes 32800 | tf_op jit(solution)/shard_map/ppermute | solution.py:297
  18.7 0.0 collective-permute-done.4.refs_5_.refs_3_
  18.7 2.0 %shard_map.85 = (f32[2,4,8,256]{3,2,1,0:T(8,128)S(1)}, bf16[2,4,8,256]{3,2,1,0:T(8,128)(2,1)S(1)}, f32[4,64,128]{2,1,0:T(8,128)S(1)}, bf16[4,64,128]{2,1,0:T(8,128)(2,1)S(1)}) custom-call(bf16[2,4,8,256]{3,2,1,0:T(8,128)(2,1)S(1)} %shard_map.79.refs_2_.refs_0_, bf16[2,4,8,256]{3,2,1,0:T(8,128)(2,1)S(1)} %collective-permute-done.1.refs_3_.refs_1_, ...), custom_call_target="tpu_custom_call" | custom-call | flops 1073741824 | bytes 65536 | tf_op jit(solution)/shard_map/pallas_call | solution.py:330
  20.8 0.1 collective-permute-start.6
  20.8 1.9 %collective-permute-start.5 = (bf16[2,4,8,256]{3,2,1,0:T(8,128)(2,1)S(1)}, bf16[2,4,8,256]{3,2,1,0:T(8,128)(2,1)S(1)}, u32[]{:S(2)}, u32[]{:S(2)}) collective-permute-start(bf16[2,4,8,256]{3,2,1,0:T(8,128)(2,1)S(1)} %get-tuple-element.28), channel_id=1, source_target_pairs={{0,1},{1,0},{2,3},{3,2},{4,5},{5,4},{6,7},{7,6},{8,9},{9,8},{10,11... | collective-permute-start | bytes 98312 | tf_op jit(solution)/shard_map/ppermute | solution.py:297
  22.8 0.0 copy-done
  22.8 2.0 %shard_map.83.refs_6_ = bf16[32,64,128]{2,1,0:T(8,128)(2,1)} custom-call(bf16[128,1024]{1,0:T(8,128)(2,1)S(1)} %get-tuple-element.22.refs_0_, f32[1,128]{1,0:T(1,128)S(1)} %bitcast.1, bf16[2,4,8,256]{3,2,1,0:T(8,128)(2,1)S(1)} %shard_map.79.refs_2_.refs_0_, bf16[2,4,8,256]{3,2,1,0:T(8,128)(2,1)S(1)} %collective-permute-done.1.refs_3_.refs_1_, ...), custom_call_target="tpu_custom_call" | custom-call | flops 536870912 | bytes 65536 | tf_op jit(solution)/shard_map/pallas_call | solution.py:330
  24.8 0.1 collective-permute-done.5.refs_1_
  24.8 0.0 collective-permute-done.6.refs_3_
  24.8 2.8 %collective-permute-start.10 = (bf16[64,128]{1,0:T(8,128)(2,1)S(1)}, bf16[64,128]{1,0:T(8,128)(2,1)S(1)}, u32[]{:S(2)}, u32[]{:S(2)}) collective-permute-start(bf16[64,128]{1,0:T(8,128)(2,1)S(1)} %get-tuple-element.36), channel_id=1, source_target_pairs={{0,24},{4,28},{8,16},{12,20},{16,8},{20,12},{24,0},{28,4},{1,25},{... | collective-permute-start | bytes 49160 | tf_op jit(solution)/shard_map/ppermute | solution.py:297
  27.6 2.6 %collective-permute-start.7 = (bf16[4,8,256]{2,1,0:T(8,128)(2,1)S(1)}, bf16[4,8,256]{2,1,0:T(8,128)(2,1)S(1)}, u32[]{:S(2)}, u32[]{:S(2)}) collective-permute-start(bf16[4,8,256]{2,1,0:T(8,128)(2,1)S(1)} %get-tuple-element.32), channel_id=1, source_target_pairs={{0,2},{1,3},{2,0},{3,1},{4,6},{5,7},{6,4},{7,5},{8,10},{9,11},{10,... | collective-permute-start | bytes 49160 | tf_op jit(solution)/shard_map/ppermute | solution.py:297
  30.2 0.5 %collective-permute-start.8 = (bf16[64,128]{1,0:T(8,128)(2,1)S(1)}, bf16[64,128]{1,0:T(8,128)(2,1)S(1)}, u32[]{:S(2)}, u32[]{:S(2)}) collective-permute-start(bf16[64,128]{1,0:T(8,128)(2,1)S(1)} %get-tuple-element.34), channel_id=1, source_target_pairs={{0,8},{4,12},{8,0},{12,4},{16,24},{20,28},{24,16},{28,20},{1,9},{5... | collective-permute-start | bytes 49160 | tf_op jit(solution)/shard_map/ppermute | solution.py:297
  30.8 0.5 %collective-permute-start.9 = (bf16[64,128]{1,0:T(8,128)(2,1)S(1)}, bf16[64,128]{1,0:T(8,128)(2,1)S(1)}, u32[]{:S(2)}, u32[]{:S(2)}) collective-permute-start(bf16[64,128]{1,0:T(8,128)(2,1)S(1)} %get-tuple-element.35), channel_id=1, source_target_pairs={{0,16},{4,20},{8,24},{12,28},{16,0},{20,4},{24,8},{28,12},{1,17},{... | collective-permute-start | bytes 49160 | tf_op jit(solution)/shard_map/ppermute | solution.py:297
  31.3 2.0 %shard_map.84 = bf16[32,64,128]{2,1,0:T(8,128)(2,1)} custom-call(bf16[128,1024]{1,0:T(8,128)(2,1)S(1)} %get-tuple-element.22.refs_0_, f32[1,128]{1,0:T(1,128)S(1)} %bitcast.2, bf16[2,4,8,256]{3,2,1,0:T(8,128)(2,1)S(1)} %shard_map.79.refs_2_.refs_0_, ...), custom_call_target="tpu_custom_call", output_to_operand_aliasing={{}: (6, {})} | custom-call | flops 536870912 | bytes 65536 | tf_op jit(solution)/shard_map/pallas_call | solution.py:330
  33.3 0.0 collective-permute-done.10.refs_5_
  33.3 0.0 collective-permute-done.7.refs_1_
  33.3 0.7 %collective-permute-done.8.refs_3_ = bf16[64,128]{1,0:T(8,128)(2,1)S(1)} collective-permute-done((bf16[64,128]{1,0:T(8,128)(2,1)S(1)}, bf16[64,128]{1,0:T(8,128)(2,1)S(1)}, u32[]{:S(2)}, u32[]{:S(2)}) %collective-permute-start.8) | collective-permute-done | bytes 16416 | tf_op jit(solution)/shard_map/ppermute | solution.py:297
  34.0 0.5 %collective-permute-done.9.refs_4_ = bf16[64,128]{1,0:T(8,128)(2,1)S(1)} collective-permute-done((bf16[64,128]{1,0:T(8,128)(2,1)S(1)}, bf16[64,128]{1,0:T(8,128)(2,1)S(1)}, u32[]{:S(2)}, u32[]{:S(2)}) %collective-permute-start.9) | collective-permute-done | bytes 16416 | tf_op jit(solution)/shard_map/ppermute | solution.py:297
  34.5 0.9 %shard_map.87 = (f32[8,32,32]{2,1,0:T(8,128)}, f32[4,32,64]{2,1,0:T(8,128)}) custom-call(f32[4,8,256]{2,1,0:T(8,128)S(1)} %get-tuple-element.31.refs_0_, bf16[4,8,256]{2,1,0:T(8,128)(2,1)S(1)} %collective-permute-done.7.refs_1_, f32[64,128]{1,0:T(8,128)S(1)} %get-tuple-element.33.refs_2_, bf16[64,128]{1,0:T(8,128)(2,1)S(1)} %collective-permute-done.8.refs_3_, ...), custom_call_target="tpu_custom_call" | custom-call | bytes 65536 | tf_op jit(solution)/shard_map/pallas_call | solution.py:330
  (3 shorter events, 0.0 us)
Async XLA Ops:
  0.6 5.4 %collective-permute-start.2 = (bf16[4,32,64]{2,1,0:T(8,128)(2,1)}, bf16[4,32,64]{2,1,0:T(8,128)(2,1)S(1)}, u32[]{:S(2)}, u32[]{:S(2)}) collective-permute-start(bf16[4,32,64]{2,1,0:T(8,128)(2,1)} %refs_1_.1), channel_id=1, source_target_pairs={{0,8},{4,12},{8,0},{12,4},{16,24},{20,28},{24,16},{28,20},{1,9},{5... | collective-permute-start | bytes 49160 | tf_op jit(solution)/shard_map/ppermute | solution.py:297
  6.1 4.0 %collective-permute-start.3 = (bf16[2,64,128]{2,1,0:T(8,128)(2,1)S(1)}, bf16[2,64,128]{2,1,0:T(8,128)(2,1)S(1)}, u32[]{:S(2)}, u32[]{:S(2)}) collective-permute-start(bf16[2,64,128]{2,1,0:T(8,128)(2,1)S(1)} %shard_map.81.one), channel_id=1, source_target_pairs={{0,16},{4,20},{8,24},{12,28},{16,0},{20,4},{24,8},{28,12},{1,17},{... | collective-permute-start | bytes 98312 | tf_op jit(solution)/shard_map/ppermute | solution.py:297
  10.1 8.6 %collective-permute-start.4 = (bf16[4,64,128]{2,1,0:T(8,128)(2,1)S(1)}, bf16[4,64,128]{2,1,0:T(8,128)(2,1)S(1)}, u32[]{:S(2)}, u32[]{:S(2)}) collective-permute-start(bf16[4,64,128]{2,1,0:T(8,128)(2,1)S(1)} %shard_map.82.refs_4_.refs_2_), channel_id=1, source_target_pairs={{0,4},{4,0},{8,12},{12,8},{16,20},{20,16},{24,28},{28,24},{1,5},{5... | collective-permute-start | bytes 196616 | tf_op jit(solution)/shard_map/ppermute | solution.py:297
  10.1 4.7 %collective-permute-start = (bf16[1,4,8,256]{3,2,1,0:T(8,128)(2,1)S(1)}, bf16[1,4,8,256]{3,2,1,0:T(8,128)(2,1)S(1)}, u32[]{:S(2)}, u32[]{:S(2)}) collective-permute-start(bf16[1,4,8,256]{3,2,1,0:T(8,128)(2,1)S(1)} %get-tuple-element.23.one), channel_id=1, source_target_pairs={{0,2},{1,3},{2,0},{3,1},{4,6},{5,7},{6,4},{7,5},{8,10},{9,11},{10,... | collective-permute-start | bytes 49160 | tf_op jit(solution)/shard_map/ppermute | solution.py:297
  14.8 8.0 %copy-start = (f32[128]{0:T(128)S(1)}, f32[128]{0:T(128)}, u32[]{:S(2)}) copy-start(f32[128]{0:T(128)} %param.8) | copy-start | bytes 1540
  14.8 3.9 %collective-permute-start.1 = (bf16[2,4,8,256]{3,2,1,0:T(8,128)(2,1)S(1)}, bf16[2,4,8,256]{3,2,1,0:T(8,128)(2,1)S(1)}, u32[]{:S(2)}, u32[]{:S(2)}) collective-permute-start(bf16[2,4,8,256]{3,2,1,0:T(8,128)(2,1)S(1)} %shard_map.79.refs_2_.refs_0_), channel_id=1, source_target_pairs={{0,1},{1,0},{2,3},{3,2},{4,5},{5,4},{6,7},{7,6},{8,9},{9,8},{10,11... | collective-permute-start | bytes 98312 | tf_op jit(solution)/shard_map/ppermute | solution.py:297
  20.8 4.1 %collective-permute-start.6 = (bf16[4,64,128]{2,1,0:T(8,128)(2,1)S(1)}, bf16[4,64,128]{2,1,0:T(8,128)(2,1)S(1)}, u32[]{:S(2)}, u32[]{:S(2)}) collective-permute-start(bf16[4,64,128]{2,1,0:T(8,128)(2,1)S(1)} %get-tuple-element.30), channel_id=1, source_target_pairs={{0,4},{4,0},{8,12},{12,8},{16,20},{20,16},{24,28},{28,24},{1,5},{5... | collective-permute-start | bytes 196616 | tf_op jit(solution)/shard_map/ppermute | solution.py:297
  20.8 4.0 %collective-permute-start.5 = (bf16[2,4,8,256]{3,2,1,0:T(8,128)(2,1)S(1)}, bf16[2,4,8,256]{3,2,1,0:T(8,128)(2,1)S(1)}, u32[]{:S(2)}, u32[]{:S(2)}) collective-permute-start(bf16[2,4,8,256]{3,2,1,0:T(8,128)(2,1)S(1)} %get-tuple-element.28), channel_id=1, source_target_pairs={{0,1},{1,0},{2,3},{3,2},{4,5},{5,4},{6,7},{7,6},{8,9},{9,8},{10,11... | collective-permute-start | bytes 98312 | tf_op jit(solution)/shard_map/ppermute | solution.py:297
  24.8 8.4 %collective-permute-start.10 = (bf16[64,128]{1,0:T(8,128)(2,1)S(1)}, bf16[64,128]{1,0:T(8,128)(2,1)S(1)}, u32[]{:S(2)}, u32[]{:S(2)}) collective-permute-start(bf16[64,128]{1,0:T(8,128)(2,1)S(1)} %get-tuple-element.36), channel_id=1, source_target_pairs={{0,24},{4,28},{8,16},{12,20},{16,8},{20,12},{24,0},{28,4},{1,25},{... | collective-permute-start | bytes 49160 | tf_op jit(solution)/shard_map/ppermute | solution.py:297
  27.6 5.6 %collective-permute-start.7 = (bf16[4,8,256]{2,1,0:T(8,128)(2,1)S(1)}, bf16[4,8,256]{2,1,0:T(8,128)(2,1)S(1)}, u32[]{:S(2)}, u32[]{:S(2)}) collective-permute-start(bf16[4,8,256]{2,1,0:T(8,128)(2,1)S(1)} %get-tuple-element.32), channel_id=1, source_target_pairs={{0,2},{1,3},{2,0},{3,1},{4,6},{5,7},{6,4},{7,5},{8,10},{9,11},{10,... | collective-permute-start | bytes 49160 | tf_op jit(solution)/shard_map/ppermute | solution.py:297
  30.2 3.7 %collective-permute-start.8 = (bf16[64,128]{1,0:T(8,128)(2,1)S(1)}, bf16[64,128]{1,0:T(8,128)(2,1)S(1)}, u32[]{:S(2)}, u32[]{:S(2)}) collective-permute-start(bf16[64,128]{1,0:T(8,128)(2,1)S(1)} %get-tuple-element.34), channel_id=1, source_target_pairs={{0,8},{4,12},{8,0},{12,4},{16,24},{20,28},{24,16},{28,20},{1,9},{5... | collective-permute-start | bytes 49160 | tf_op jit(solution)/shard_map/ppermute | solution.py:297
  30.8 3.7 %collective-permute-start.9 = (bf16[64,128]{1,0:T(8,128)(2,1)S(1)}, bf16[64,128]{1,0:T(8,128)(2,1)S(1)}, u32[]{:S(2)}, u32[]{:S(2)}) collective-permute-start(bf16[64,128]{1,0:T(8,128)(2,1)S(1)} %get-tuple-element.35), channel_id=1, source_target_pairs={{0,16},{4,20},{8,24},{12,28},{16,0},{20,4},{24,8},{28,12},{1,17},{... | collective-permute-start | bytes 49160 | tf_op jit(solution)/shard_map/ppermute | solution.py:297

commit v2 on v1

--- a/solution.py
+++ b/solution.py
@@ -84,6 +84,13 @@
         out[s * half : (s + 1) * half, :] = jnp.concatenate(block, axis=1).astype(out.dtype)
 
 
+def left_layout(ref, out):
+    part, channels, tile_rows = ref.shape
+    flat = ref[...].astype(jnp.float32).reshape(part * channels, tile_rows).T
+    for n in range(out.shape[0]):
+        out[n] = block_transpose(flat[n * part : (n + 1) * part]).astype(out.dtype)
+
+
 def prepare_kernel(inside, *refs):
     sources, (left_out, *outs), (left_ref, sent) = refs[:4], refs[4:8], refs[8:]
     moves = [
@@ -94,11 +101,7 @@
         move.start()
     moves[0].wait()
     if inside:
-        part, channels, tile_rows = left_ref.shape
-        flat = left_ref[...].astype(jnp.float32).reshape(part * channels, tile_rows).T
-        for n in range(left_out.shape[1]):
-            piece = block_transpose(flat[n * part : (n + 1) * part])
-            left_out[0, n] = piece.astype(left_out.dtype)
+        left_layout(left_ref, left_out.at[0])
     else:
         left_out[0] = left_ref[...]
     for move in moves[1:]:
@@ -114,10 +117,10 @@
     transposed_ref[...] = flat.astype(jnp.float32).T.astype(jnp.bfloat16)
 
 
-def stack_kernel(raw, one, other, *refs):
+def stack_kernel(change, one, other, *refs):
     out = refs[-1]
     count = out.shape[0] // 2
-    if raw:
+    if change is dense:
         dense(one, out.at[0])
         dense(other, out.at[1])
     else:
@@ -214,29 +217,27 @@
                 ref[n, copy] = left_f32[copy, place ^ key].astype(ref.dtype)
 
 
-def forward_kernel(sizes, left_keys, right_keys, first, aliased, *refs):
+def forward_kernel(sizes, left_keys, right_keys, *refs):
     rows, channels, copies, groups, columns = sizes
     n_left, n_right = len(left_keys), len(right_keys)
     weight_ref, bias_ref, refs = refs[0], refs[1], refs[2:]
     left_refs, refs = list(zip(refs[:n_left], left_keys)), refs[n_left:]
     right_refs, refs = list(zip(refs[:n_right], right_keys)), refs[n_right:]
-    out_ref, left_f32, right_f32, outer_t, pairs, sent = refs[1:] if aliased else refs
-    count = outer_t.shape[0]
+    out_ref, left_f32, right_f32, outer_t = refs
     place_right(right_refs, right_f32)
     left_t = place_left(left_refs, left_f32).T.astype(jnp.bfloat16)
-    left_t = left_t[first * channels : (first + count) * channels]
     pack = LANES // columns
     half = channels // pack
     scale = 1.0 / rows
     bias = bias_ref[...]
-    small = count <= 8
+    small = groups <= 8
 
     def e_step(start):
         diag = block_diagonal(right_f32, start, rows, channels, columns, copies)
         for h in range(pack):
             outer = (dot(left_t, diag[h], NN) * scale).astype(jnp.bfloat16)
             at = pl.ds((start + h * half) * channels, channels)
-            for g in range(count):
+            for g in range(groups):
                 outer_t[g, at, :] = outer[g * channels : (g + 1) * channels]
 
     loop(half, e_step, small)
@@ -245,33 +246,25 @@
         pair = dot(weight_ref[...], outer_t[g], NN).T + bias
         pair = pair.astype(jnp.bfloat16)
         for n in range(copies):
-            pairs[n * count + g] = pair[n * columns : (n + 1) * columns]
-
-    loop(count, g_step, small)
-    moves = []
-    for n in range(copies):
-        source = pairs.at[pl.ds(n * count, count)]
-        target = out_ref.at[pl.ds(n * groups + first, count)]
-        moves.append(pltpu.make_async_copy(source, target, sent.at[n]))
-        moves[-1].start()
-    for move in moves:
-        move.wait()
-
-
-def add_kernel(*refs):
-    (left_kept, left_new, right_kept, right_new), outs = refs[:4], refs[4:]
-    for n in range(left_kept.shape[0]):
-        total = left_kept[n] + left_new[n].astype(jnp.float32)
-        outs[n][...] = total.astype(outs[n].dtype)
-    outs = outs[left_kept.shape[0] :]
-    for n in range(right_kept.shape[0]):
-        total = right_kept[n] + right_new[n].astype(jnp.float32)
-        outs[n][...] = total.astype(outs[n].dtype)
-
-
-def sum_kernel(n_left, inside, *refs):
+            out_ref[n * groups + g] = pair[n * columns : (n + 1) * columns]
+
+    loop(groups, g_step, small)
+
+
+def add_kernel(kept, new, *outs):
+    for n, out in enumerate(outs):
+        out[...] = (kept[n] + new[n].astype(jnp.float32)).astype(out.dtype)
+
+
+def last_kernel(n_left, n_right, inside, pairs, *refs):
     left_refs, refs = refs[:n_left], refs[n_left:]
-    right_refs, (left_out, right_out) = refs[:-2], refs[-2:]
+    right_refs, refs = refs[:n_right], refs[n_right:]
+    outs, (left_out, right_out, sent) = refs[:3], refs[3:]
+    moves = [
+        pltpu.make_async_copy(source, target, sent.at[n])
+        for n, (source, target) in enumerate(zip((pairs, left_out, right_out), outs))
+    ]
+    moves[0].start()
     total = left_refs[0][...]
     for ref in left_refs[1:]:
         total = total + ref[...].astype(jnp.float32)
@@ -280,6 +273,7 @@
         left_out[...] = total.T.reshape(left_out.shape)
     else:
         left_out[...] = total
+    moves[1].start()
     total = right_refs[0][...]
     for ref in right_refs[1:]:
         total = total + ref[...].astype(jnp.float32)
@@ -290,6 +284,9 @@
         part = total[s * half : (s + 1) * half]
         for h in range(pack):
             right_out[s, h * half : (h + 1) * half, :] = part[:, h * columns : (h + 1) * columns]
+    moves[2].start()
+    for move in moves:
+        move.wait()
 
 
 def exchange(x, axis, m):
@@ -344,6 +341,7 @@
     hbm = functools.partial(pltpu.with_memory_space_constraint, memory_space=pltpu.HBM)
 
     steps = powers(n_wide)[1:] + [1]
+    narrow_steps = powers(n_narrow)[::-1]
     right_new = exchange(right, "wide", steps[0])
     source = left
     if not inside:
@@ -366,12 +364,14 @@
         cost=flops // 8,
     )
 
-    def stack(one, other, raw, after=()):
-        shapes = right_shape if raw else one.shape[1:]
-        outs = [shape((2 if raw else 2 * one.shape[0],) + shapes, bf16)]
+    def stack(one, other, change, after=()):
+        total, shapes = 2 * one.shape[0], one.shape[1:]
+        if change is dense:
+            total, shapes = 2, right_shape
         args = [one, other, *after]
         specs = vmem(2) + [anywhere] * len(after)
-        return call(functools.partial(stack_kernel, raw), outs, args, in_specs=specs)[0]
+        kernel = functools.partial(stack_kernel, change)
+        return call(kernel, [shape((total,) + shapes, bf16)], args, in_specs=specs)[0]
 
     d_shape = shape((channels, count * channels, copies * columns), bf16)
     d_outer = []
@@ -385,17 +385,17 @@
             right_new = exchange(rights, "wide", m)
         new = [k ^ m for k in keys]
         if n + 1 < len(steps):
-            rights = stack(rights, right_new, n == 0, d_outer[n : n + 1])
+            change = dense if n == 0 else None
+            rights = stack(rights, right_new, change, d_outer[n : n + 1])
             keys = keys + new
     right_keys, rights = (keys, new), [rights, right_new]
 
     keys = [0]
-    steps = powers(n_narrow)[::-1]
-    for n, m in enumerate(steps):
+    for n, m in enumerate(narrow_steps):
         left_new = exchange(lefts, "narrow", m)
         new = [k ^ m for k in keys]
-        if n + 1 < len(steps):
-            lefts = stack(lefts, left_new, False, d_outer[1:2] if n == 0 else ())
+        if n + 1 < len(narrow_steps):
+            lefts = stack(lefts, left_new, None)
             keys = keys + new
     left_keys, lefts = (keys, new), [lefts, left_new]
 
@@ -422,50 +422,35 @@
     left_new = exchange(left_sent, "narrow", 1)
     right_new = exchange(right_sent, "wide", 1)
 
-    def forward(first, before):
-        args = [transposed, out_bias.reshape(1, width), *lefts, *rights]
-        specs, more = vmem(len(args)), {}
-        if before is not None:
-            more = {"input_output_aliases": {len(args): 0}}
-            args, specs = args + [before], specs + [anywhere]
-        return call(
-            functools.partial(
-                forward_kernel, sizes, left_keys, right_keys, first, before is not None
-            ),
-            [shape(cotangent.shape, bf16)],
-            args,
-            [
-                left_f32,
-                right_f32,
-                pltpu.VMEM((count, channels * channels, copies * columns), bf16),
-                pltpu.VMEM((copies * count, columns, width), bf16),
-                pltpu.SemaphoreType.DMA((copies,)),
-            ],
-            cost=flops,
-            in_specs=specs,
-            out_specs=[anywhere],
-            **more,
-        )[0]
-
-    pair_update = forward(0, None)
-    sums = call(
-        add_kernel,
-        [shape(left_shape, bf16 if n else f32) for n in range(far)]
-        + [shape(right_shape, bf16 if n else f32) for n in range(near)],
-        [left_kept, left_new, right_kept, right_new],
-    )
-    left_sums = [exchange(v, "narrow", 2 * n) if n else v for n, v in enumerate(sums[:far])]
-    right_sums = [exchange(v, "wide", 2 * n) if n else v for n, v in enumerate(sums[far:])]
-    for n in range(1, halves):
-        pair_update = forward(n * count, pair_update)
-
-    grad_left, grad_right = call(
-        functools.partial(sum_kernel, far, inside),
-        [
-            shape((part, channels, tile_rows) if inside else left_shape, f32),
-            shape((right_part, channels, columns), f32),
-        ],
-        [*left_sums, *right_sums],
+    def add(kept, new):
+        outs = [shape(kept.shape[1:], bf16 if n else f32) for n in range(kept.shape[0])]
+        return list(call(add_kernel, outs, [kept, new]))
+
+    right_sums = add(right_kept, right_new)
+    for n in range(1, near):
+        right_sums[n] = exchange(right_sums[n], "wide", 2 * n)
+    left_sums = add(left_kept, left_new)
+    for n in range(1, far):
+        left_sums[n] = exchange(left_sums[n], "narrow", 2 * n)
+
+    (pairs,) = call(
+        functools.partial(forward_kernel, sizes, left_keys, right_keys),
+        [shape(cotangent.shape, bf16)],
+        [transposed, out_bias.reshape(1, width), *lefts, *rights],
+        [left_f32, right_f32, pltpu.VMEM((groups, channels * channels, copies * columns), bf16)],
+        cost=2 * flops,
+    )
+    last = [
+        shape(cotangent.shape, bf16),
+        shape((part, channels, tile_rows) if inside else left_shape, f32),
+        shape((right_part, channels, columns), f32),
+    ]
+    pair_update, grad_left, grad_right = call(
+        functools.partial(last_kernel, far, near, inside),
+        last,
+        [pairs, *left_sums, *right_sums],
+        [pltpu.VMEM(v.shape, f32) for v in last[1:]] + [pltpu.SemaphoreType.DMA((3,))],
+        out_specs=[outside] * 3,
     )
     if not inside:
         grad_left = grad_left.reshape(copies, part, groups, channels).transpose(1, 3, 0, 2)

time: 35.5 us -> 35.7 us (level)
  waiting for transfers between devices: 6.5 us -> 8.44 us
  Pallas kernels: 10 us -> 8.17 us
    ppermute x11, waiting for transfers between devices: 6.5 us -> 8.44 us  [exchange(): return lax.ppermute(x, axis, [(n, n ^ m) for n in range(size)])]
    pallas_call x12, Pallas kernels: 10 us -> 8.17 us  [call(): pl.pallas_call(kernel, in_specs=in_specs or vmem(len(args)), out_specs=ou...]
  transfers between devices with their start and end apart: 11 -> 11, of which waited for: 6 -> 6; matrix products, arithmetic and copies ran while one was open for 0% -> 0% of each run, Pallas kernels for 20% -> 14%
where the time goes in v2:
time: 35.7 us; the launch traced here: 35.5 us
  starting transfers between devices  18.2 us (51%)
  waiting for transfers between devices  8.44 us (24%)
  Pallas kernels  8.17 us (23%)
  between operations  0.74 us (2%)
    ppermute x11, starting transfers between devices, exchange(): return lax.ppermute(x, axis, [(n, n ^ m) for n in range(size)])  18.2 us
    ppermute x11, waiting for transfers between devices, exchange(): return lax.ppermute(x, axis, [(n, n ^ m) for n in range(size)])  8.44 us
    pallas_call x12, Pallas kernels, call(): pl.pallas_call(kernel, in_specs=in_specs or vmem(len(args)), out_specs=ou...  8.17 us
  transfers between devices with their start and end apart: 11, of which 6 were waited for; matrix products, arithmetic and copies ran while one was open for 0% of the time, Pallas kernels for 14%

profile of v2, /device:TPU:0, one launch (start us, length us, event | category | flops | bytes accessed | tf_op | source)
XLA Modules:
  0.0 35.5 jit_solution(11291365662101961202)
XLA Ops:
  0.6 3.0 %collective-permute-start.2 = (bf16[4,32,64]{2,1,0:T(8,128)(2,1)}, bf16[4,32,64]{2,1,0:T(8,128)(2,1)S(1)}, u32[]{:S(2)}, u32[]{:S(2)}) collective-permute-start(bf16[4,32,64]{2,1,0:T(8,128)(2,1)} %refs_1_.1), channel_id=1, source_target_pairs={{0,8},{4,12},{8,0},{12,4},{16,24},{20,28},{24,16},{28,20},{1,9},{5... | collective-permute-start | bytes 49160 | tf_op jit(solution)/shard_map/ppermute | solution.py:294
  3.7 1.2 %shard_map.76 = (bf16[1,4,8,256]{3,2,1,0:T(8,128)(2,1)S(1)}, bf16[4,32,64]{2,1,0:T(8,128)(2,1)S(1)}, bf16[1024,128]{1,0:T(8,128)(2,1)S(1)}, bf16[32,64,128]{2,1,0:T(8,128)(2,1)S(1)}) custom-call(bf16[8,32,32]{2,1,0:T(8,128)(2,1)} %refs_0_.1, bf16[4,32,64]{2,1,0:T(8,128)(2,1)} %refs_1_.1, bf16[1024,128]{1,0:T(8,128)(2,1)} %refs_2_.1, bf16[32,64,128]{2,1,0:T(8,128)(2,1)} %refs_3_.1), custom_call_target="tpu_custom_call" | custom-call | flops 33554432 | bytes 65536 | tf_op jit(solution)/shard_map/pallas_call | solution.py:327
  4.9 0.4 %shard_map.77 = (bf16[32,32,128]{2,1,0:T(8,128)(2,1)S(1)}, bf16[128,1024]{1,0:T(8,128)(2,1)S(1)}) custom-call(bf16[1024,128]{1,0:T(8,128)(2,1)S(1)} %get-tuple-element.19.weight_ref), custom_call_target="tpu_custom_call" | custom-call | flops 67108864 | bytes 65536 | tf_op jit(solution)/shard_map/pallas_call | solution.py:327
  5.3 0.7 %shard_map.79.refs_0_.refs_4_ = bf16[32,128,256]{2,1,0:T(8,128)(2,1)S(1)} custom-call(bf16[32,64,128]{2,1,0:T(8,128)(2,1)S(1)} %get-tuple-element.23.cot_ref, bf16[32,32,128]{2,1,0:T(8,128)(2,1)S(1)} %get-tuple-element.24.weight_ref), custom_call_target="tpu_custom_call" | custom-call | flops 268435456 | bytes 65536 | tf_op jit(solution)/shard_map/pallas_call | solution.py:327
  6.0 0.0 collective-permute-done.2.other
  6.0 0.1 shard_map.80.one
  6.1 1.9 %collective-permute-start.3 = (bf16[2,64,128]{2,1,0:T(8,128)(2,1)S(1)}, bf16[2,64,128]{2,1,0:T(8,128)(2,1)S(1)}, u32[]{:S(2)}, u32[]{:S(2)}) collective-permute-start(bf16[2,64,128]{2,1,0:T(8,128)(2,1)S(1)} %shard_map.80.one), channel_id=1, source_target_pairs={{0,16},{4,20},{8,24},{12,28},{16,0},{20,4},{24,8},{28,12},{1,17},{... | collective-permute-start | bytes 98312 | tf_op jit(solution)/shard_map/ppermute | solution.py:294
  8.0 0.7 %shard_map.81.refs_0_.refs_5_ = bf16[32,128,256]{2,1,0:T(8,128)(2,1)S(1)} custom-call(bf16[32,64,128]{2,1,0:T(8,128)(2,1)S(1)} %get-tuple-element.23.cot_ref, bf16[32,32,128]{2,1,0:T(8,128)(2,1)S(1)} %get-tuple-element.24.weight_ref), custom_call_target="tpu_custom_call" | custom-call | flops 268435456 | bytes 65536 | tf_op jit(solution)/shard_map/pallas_call | solution.py:327
  8.7 1.4 %collective-permute-done.3.other = bf16[2,64,128]{2,1,0:T(8,128)(2,1)S(1)} collective-permute-done((bf16[2,64,128]{2,1,0:T(8,128)(2,1)S(1)}, bf16[2,64,128]{2,1,0:T(8,128)(2,1)S(1)}, u32[]{:S(2)}, u32[]{:S(2)}) %collective-permute-start.3) | collective-permute-done | bytes 32800 | tf_op jit(solution)/shard_map/ppermute | solution.py:294
  10.1 0.0 collective-permute-start.4
  10.1 2.9 %collective-permute-start = (bf16[1,4,8,256]{3,2,1,0:T(8,128)(2,1)S(1)}, bf16[1,4,8,256]{3,2,1,0:T(8,128)(2,1)S(1)}, u32[]{:S(2)}, u32[]{:S(2)}) collective-permute-start(bf16[1,4,8,256]{3,2,1,0:T(8,128)(2,1)S(1)} %get-tuple-element.21.one), channel_id=1, source_target_pairs={{0,2},{1,3},{2,0},{3,1},{4,6},{5,7},{6,4},{7,5},{8,10},{9,11},{10,... | collective-permute-start | bytes 49160 | tf_op jit(solution)/shard_map/ppermute | solution.py:294
  13.0 1.8 %collective-permute-done.other = bf16[1,4,8,256]{3,2,1,0:T(8,128)(2,1)S(1)} collective-permute-done((bf16[1,4,8,256]{3,2,1,0:T(8,128)(2,1)S(1)}, bf16[1,4,8,256]{3,2,1,0:T(8,128)(2,1)S(1)}, u32[]{:S(2)}, u32[]{:S(2)}) %collective-permute-start) | collective-permute-done | bytes 16416 | tf_op jit(solution)/shard_map/ppermute | solution.py:294
  14.8 0.0 copy-start
  14.8 1.9 %collective-permute-start.1 = (bf16[2,4,8,256]{3,2,1,0:T(8,128)(2,1)S(1)}, bf16[2,4,8,256]{3,2,1,0:T(8,128)(2,1)S(1)}, u32[]{:S(2)}, u32[]{:S(2)}) collective-permute-start(bf16[2,4,8,256]{3,2,1,0:T(8,128)(2,1)S(1)} %shard_map.78.refs_2_.refs_0_), channel_id=1, source_target_pairs={{0,1},{1,0},{2,3},{3,2},{4,5},{5,4},{6,7},{7,6},{8,9},{9,8},{10,11... | collective-permute-start | bytes 98312 | tf_op jit(solution)/shard_map/ppermute | solution.py:294
  16.7 2.1 %collective-permute-done.1.refs_3_.refs_1_ = bf16[2,4,8,256]{3,2,1,0:T(8,128)(2,1)S(1)} collective-permute-done((bf16[2,4,8,256]{3,2,1,0:T(8,128)(2,1)S(1)}, bf16[2,4,8,256]{3,2,1,0:T(8,128)(2,1)S(1)}, u32[]{:S(2)}, u32[]{:S(2)}) %collective-permute-start.1) | collective-permute-done | bytes 32800 | tf_op jit(solution)/shard_map/ppermute | solution.py:294
  18.7 0.0 collective-permute-done.4.refs_5_.refs_3_
  18.7 2.0 %shard_map.84 = (f32[2,4,8,256]{3,2,1,0:T(8,128)S(1)}, bf16[2,4,8,256]{3,2,1,0:T(8,128)(2,1)S(1)}, f32[4,64,128]{2,1,0:T(8,128)S(1)}, bf16[4,64,128]{2,1,0:T(8,128)(2,1)S(1)}) custom-call(bf16[2,4,8,256]{3,2,1,0:T(8,128)(2,1)S(1)} %shard_map.78.refs_2_.refs_0_, bf16[2,4,8,256]{3,2,1,0:T(8,128)(2,1)S(1)} %collective-permute-done.1.refs_3_.refs_1_, ...), custom_call_target="tpu_custom_call" | custom-call | flops 1073741824 | bytes 65536 | tf_op jit(solution)/shard_map/pallas_call | solution.py:327
  20.8 0.1 collective-permute-start.7
  20.8 1.9 %collective-permute-start.5 = (bf16[2,4,8,256]{3,2,1,0:T(8,128)(2,1)S(1)}, bf16[2,4,8,256]{3,2,1,0:T(8,128)(2,1)S(1)}, u32[]{:S(2)}, u32[]{:S(2)}) collective-permute-start(bf16[2,4,8,256]{3,2,1,0:T(8,128)(2,1)S(1)} %get-tuple-element.26), channel_id=1, source_target_pairs={{0,1},{1,0},{2,3},{3,2},{4,5},{5,4},{6,7},{7,6},{8,9},{9,8},{10,11... | collective-permute-start | bytes 98312 | tf_op jit(solution)/shard_map/ppermute | solution.py:294
  22.8 2.1 %collective-permute-done.5.new = bf16[2,4,8,256]{3,2,1,0:T(8,128)(2,1)S(1)} collective-permute-done((bf16[2,4,8,256]{3,2,1,0:T(8,128)(2,1)S(1)}, bf16[2,4,8,256]{3,2,1,0:T(8,128)(2,1)S(1)}, u32[]{:S(2)}, u32[]{:S(2)}) %collective-permute-start.5) | collective-permute-done | bytes 32800 | tf_op jit(solution)/shard_map/ppermute | solution.py:294
  24.8 2.9 %collective-permute-start.6 = (bf16[4,8,256]{2,1,0:T(8,128)(2,1)S(1)}, bf16[4,8,256]{2,1,0:T(8,128)(2,1)S(1)}, u32[]{:S(2)}, u32[]{:S(2)}) collective-permute-start(bf16[4,8,256]{2,1,0:T(8,128)(2,1)S(1)} %get-tuple-element.28), channel_id=1, source_target_pairs={{0,2},{1,3},{2,0},{3,1},{4,6},{5,7},{6,4},{7,5},{8,10},{9,11},{10,... | collective-permute-start | bytes 49160 | tf_op jit(solution)/shard_map/ppermute | solution.py:294
  27.8 0.0 collective-permute-done.7.new
  27.8 2.5 %collective-permute-start.10 = (bf16[64,128]{1,0:T(8,128)(2,1)S(1)}, bf16[64,128]{1,0:T(8,128)(2,1)S(1)}, u32[]{:S(2)}, u32[]{:S(2)}) collective-permute-start(bf16[64,128]{1,0:T(8,128)(2,1)S(1)} %get-tuple-element.34), channel_id=1, source_target_pairs={{0,24},{4,28},{8,16},{12,20},{16,8},{20,12},{24,0},{28,4},{1,25},{... | collective-permute-start | bytes 49160 | tf_op jit(solution)/shard_map/ppermute | solution.py:294
  30.3 0.5 %collective-permute-start.8 = (bf16[64,128]{1,0:T(8,128)(2,1)S(1)}, bf16[64,128]{1,0:T(8,128)(2,1)S(1)}, u32[]{:S(2)}, u32[]{:S(2)}) collective-permute-start(bf16[64,128]{1,0:T(8,128)(2,1)S(1)} %get-tuple-element.32), channel_id=1, source_target_pairs={{0,8},{4,12},{8,0},{12,4},{16,24},{20,28},{24,16},{28,20},{1,9},{5... | collective-permute-start | bytes 49160 | tf_op jit(solution)/shard_map/ppermute | solution.py:294
  30.8 0.5 %collective-permute-start.9 = (bf16[64,128]{1,0:T(8,128)(2,1)S(1)}, bf16[64,128]{1,0:T(8,128)(2,1)S(1)}, u32[]{:S(2)}, u32[]{:S(2)}) collective-permute-start(bf16[64,128]{1,0:T(8,128)(2,1)S(1)} %get-tuple-element.33), channel_id=1, source_target_pairs={{0,16},{4,20},{8,24},{12,28},{16,0},{20,4},{24,8},{28,12},{1,17},{... | collective-permute-start | bytes 49160 | tf_op jit(solution)/shard_map/ppermute | solution.py:294
  31.3 0.0 copy-done
  31.3 2.1 %shard_map.83.pairs = bf16[32,64,128]{2,1,0:T(8,128)(2,1)S(1)} custom-call(bf16[128,1024]{1,0:T(8,128)(2,1)S(1)} %get-tuple-element.20.refs_0_, f32[1,128]{1,0:T(1,128)S(1)} %bitcast.1, bf16[2,4,8,256]{3,2,1,0:T(8,128)(2,1)S(1)} %shard_map.78.refs_2_.refs_0_, bf16[2,4,8,256]{3,2,1,0:T(8,128)(2,1)S(1)} %collective-permute-done.1.refs_3_.refs_1_, ...), custom_call_target="tpu_custom_call" | custom-call | flops 1073741824 | bytes 65536 | tf_op jit(solution)/shard_map/pallas_call | solution.py:327
  33.4 0.0 collective-permute-done.6.refs_1_
  33.4 0.0 collective-permute-done.10.refs_5_
  33.4 0.6 %collective-permute-done.8.refs_3_ = bf16[64,128]{1,0:T(8,128)(2,1)S(1)} collective-permute-done((bf16[64,128]{1,0:T(8,128)(2,1)S(1)}, bf16[64,128]{1,0:T(8,128)(2,1)S(1)}, u32[]{:S(2)}, u32[]{:S(2)}) %collective-permute-start.8) | collective-permute-done | bytes 16416 | tf_op jit(solution)/shard_map/ppermute | solution.py:294
  34.0 0.5 %collective-permute-done.9.refs_4_ = bf16[64,128]{1,0:T(8,128)(2,1)S(1)} collective-permute-done((bf16[64,128]{1,0:T(8,128)(2,1)S(1)}, bf16[64,128]{1,0:T(8,128)(2,1)S(1)}, u32[]{:S(2)}, u32[]{:S(2)}) %collective-permute-start.9) | collective-permute-done | bytes 16416 | tf_op jit(solution)/shard_map/ppermute | solution.py:294
  34.6 1.0 %shard_map.87 = (bf16[32,64,128]{2,1,0:T(8,128)(2,1)}, f32[8,32,32]{2,1,0:T(8,128)}, f32[4,32,64]{2,1,0:T(8,128)}) custom-call(bf16[32,64,128]{2,1,0:T(8,128)(2,1)S(1)} %shard_map.83.pairs, f32[4,8,256]{2,1,0:T(8,128)S(1)} %get-tuple-element.27.refs_0_, bf16[4,8,256]{2,1,0:T(8,128)(2,1)S(1)} %collective-permute-done.6.refs_1_, ...), custom_call_target="tpu_custom_call" | custom-call | bytes 65536 | tf_op jit(solution)/shard_map/pallas_call | solution.py:327
  (4 shorter events, 0.0 us)
Async XLA Ops:
  0.6 5.4 %collective-permute-start.2 = (bf16[4,32,64]{2,1,0:T(8,128)(2,1)}, bf16[4,32,64]{2,1,0:T(8,128)(2,1)S(1)}, u32[]{:S(2)}, u32[]{:S(2)}) collective-permute-start(bf16[4,32,64]{2,1,0:T(8,128)(2,1)} %refs_1_.1), channel_id=1, source_target_pairs={{0,8},{4,12},{8,0},{12,4},{16,24},{20,28},{24,16},{28,20},{1,9},{5... | collective-permute-start | bytes 49160 | tf_op jit(solution)/shard_map/ppermute | solution.py:294
  6.1 4.0 %collective-permute-start.3 = (bf16[2,64,128]{2,1,0:T(8,128)(2,1)S(1)}, bf16[2,64,128]{2,1,0:T(8,128)(2,1)S(1)}, u32[]{:S(2)}, u32[]{:S(2)}) collective-permute-start(bf16[2,64,128]{2,1,0:T(8,128)(2,1)S(1)} %shard_map.80.one), channel_id=1, source_target_pairs={{0,16},{4,20},{8,24},{12,28},{16,0},{20,4},{24,8},{28,12},{1,17},{... | collective-permute-start | bytes 98312 | tf_op jit(solution)/shard_map/ppermute | solution.py:294
  10.1 8.6 %collective-permute-start.4 = (bf16[4,64,128]{2,1,0:T(8,128)(2,1)S(1)}, bf16[4,64,128]{2,1,0:T(8,128)(2,1)S(1)}, u32[]{:S(2)}, u32[]{:S(2)}) collective-permute-start(bf16[4,64,128]{2,1,0:T(8,128)(2,1)S(1)} %shard_map.82.refs_4_.refs_2_), channel_id=1, source_target_pairs={{0,4},{4,0},{8,12},{12,8},{16,20},{20,16},{24,28},{28,24},{1,5},{5... | collective-permute-start | bytes 196616 | tf_op jit(solution)/shard_map/ppermute | solution.py:294
  10.1 4.7 %collective-permute-start = (bf16[1,4,8,256]{3,2,1,0:T(8,128)(2,1)S(1)}, bf16[1,4,8,256]{3,2,1,0:T(8,128)(2,1)S(1)}, u32[]{:S(2)}, u32[]{:S(2)}) collective-permute-start(bf16[1,4,8,256]{3,2,1,0:T(8,128)(2,1)S(1)} %get-tuple-element.21.one), channel_id=1, source_target_pairs={{0,2},{1,3},{2,0},{3,1},{4,6},{5,7},{6,4},{7,5},{8,10},{9,11},{10,... | collective-permute-start | bytes 49160 | tf_op jit(solution)/shard_map/ppermute | solution.py:294
  14.8 16.5 %copy-start = (f32[128]{0:T(128)S(1)}, f32[128]{0:T(128)}, u32[]{:S(2)}) copy-start(f32[128]{0:T(128)} %param.8) | copy-start | bytes 1540
  14.8 3.9 %collective-permute-start.1 = (bf16[2,4,8,256]{3,2,1,0:T(8,128)(2,1)S(1)}, bf16[2,4,8,256]{3,2,1,0:T(8,128)(2,1)S(1)}, u32[]{:S(2)}, u32[]{:S(2)}) collective-permute-start(bf16[2,4,8,256]{3,2,1,0:T(8,128)(2,1)S(1)} %shard_map.78.refs_2_.refs_0_), channel_id=1, source_target_pairs={{0,1},{1,0},{2,3},{3,2},{4,5},{5,4},{6,7},{7,6},{8,9},{9,8},{10,11... | collective-permute-start | bytes 98312 | tf_op jit(solution)/shard_map/ppermute | solution.py:294
  20.8 7.0 %collective-permute-start.7 = (bf16[4,64,128]{2,1,0:T(8,128)(2,1)S(1)}, bf16[4,64,128]{2,1,0:T(8,128)(2,1)S(1)}, u32[]{:S(2)}, u32[]{:S(2)}) collective-permute-start(bf16[4,64,128]{2,1,0:T(8,128)(2,1)S(1)} %get-tuple-element.30), channel_id=1, source_target_pairs={{0,4},{4,0},{8,12},{12,8},{16,20},{20,16},{24,28},{28,24},{1,5},{5... | collective-permute-start | bytes 196616 | tf_op jit(solution)/shard_map/ppermute | solution.py:294
  20.8 4.0 %collective-permute-start.5 = (bf16[2,4,8,256]{3,2,1,0:T(8,128)(2,1)S(1)}, bf16[2,4,8,256]{3,2,1,0:T(8,128)(2,1)S(1)}, u32[]{:S(2)}, u32[]{:S(2)}) collective-permute-start(bf16[2,4,8,256]{3,2,1,0:T(8,128)(2,1)S(1)} %get-tuple-element.26), channel_id=1, source_target_pairs={{0,1},{1,0},{2,3},{3,2},{4,5},{5,4},{6,7},{7,6},{8,9},{9,8},{10,11... | collective-permute-start | bytes 98312 | tf_op jit(solution)/shard_map/ppermute | solution.py:294
  24.8 8.6 %collective-permute-start.6 = (bf16[4,8,256]{2,1,0:T(8,128)(2,1)S(1)}, bf16[4,8,256]{2,1,0:T(8,128)(2,1)S(1)}, u32[]{:S(2)}, u32[]{:S(2)}) collective-permute-start(bf16[4,8,256]{2,1,0:T(8,128)(2,1)S(1)} %get-tuple-element.28), channel_id=1, source_target_pairs={{0,2},{1,3},{2,0},{3,1},{4,6},{5,7},{6,4},{7,5},{8,10},{9,11},{10,... | collective-permute-start | bytes 49160 | tf_op jit(solution)/shard_map/ppermute | solution.py:294
  27.8 5.6 %collective-permute-start.10 = (bf16[64,128]{1,0:T(8,128)(2,1)S(1)}, bf16[64,128]{1,0:T(8,128)(2,1)S(1)}, u32[]{:S(2)}, u32[]{:S(2)}) collective-permute-start(bf16[64,128]{1,0:T(8,128)(2,1)S(1)} %get-tuple-element.34), channel_id=1, source_target_pairs={{0,24},{4,28},{8,16},{12,20},{16,8},{20,12},{24,0},{28,4},{1,25},{... | collective-permute-start | bytes 49160 | tf_op jit(solution)/shard_map/ppermute | solution.py:294
  30.3 3.7 %collective-permute-start.8 = (bf16[64,128]{1,0:T(8,128)(2,1)S(1)}, bf16[64,128]{1,0:T(8,128)(2,1)S(1)}, u32[]{:S(2)}, u32[]{:S(2)}) collective-permute-start(bf16[64,128]{1,0:T(8,128)(2,1)S(1)} %get-tuple-element.32), channel_id=1, source_target_pairs={{0,8},{4,12},{8,0},{12,4},{16,24},{20,28},{24,16},{28,20},{1,9},{5... | collective-permute-start | bytes 49160 | tf_op jit(solution)/shard_map/ppermute | solution.py:294
  30.8 3.7 %collective-permute-start.9 = (bf16[64,128]{1,0:T(8,128)(2,1)S(1)}, bf16[64,128]{1,0:T(8,128)(2,1)S(1)}, u32[]{:S(2)}, u32[]{:S(2)}) collective-permute-start(bf16[64,128]{1,0:T(8,128)(2,1)S(1)} %get-tuple-element.33), channel_id=1, source_target_pairs={{0,16},{4,20},{8,24},{12,28},{16,0},{20,4},{24,8},{28,12},{1,17},{... | collective-permute-start | bytes 49160 | tf_op jit(solution)/shard_map/ppermute | solution.py:294

commit v3 on v2

--- a/solution.py
+++ b/solution.py
@@ -146,20 +146,56 @@
     loop(count, step, count <= 8)
 
 
-def gradient_kernel(sizes, left_keys, right_keys, *refs):
+def split_parts(total, axis, kept_ref, sent_ref):
+    place = lax.axis_index(axis)
+    for n in range(kept_ref.shape[0]):
+        kept_ref[n] = total(place ^ (2 * n)).astype(kept_ref.dtype)
+        sent_ref[n] = total(place ^ (2 * n + 1)).astype(sent_ref.dtype)
+
+
+def left_gradient_kernel(sizes, right_keys, *refs):
+    rows, channels, copies, groups, columns = sizes
+    n_right = len(right_keys)
+    right_refs, refs = list(zip(refs[:n_right], right_keys)), refs[n_right:]
+    d_refs, (kept_ref, sent_ref, left_f32, right_f32, left_sum) = refs[:-5], refs[-5:]
+    place_right(right_refs, right_f32)
+    pack = LANES // columns
+    half = channels // pack
+    small = groups * channels <= MXU
+    if not small:
+        left_sum[...] = jnp.zeros_like(left_sum)
+    totals = []
+
+    def step(first):
+        diag = block_diagonal(right_f32, first, rows, channels, columns, copies)
+        for h in range(pack):
+            d_e = jnp.concatenate([ref[first + h * half] for ref in d_refs], axis=0)
+            term = dot(d_e, diag[h], NT)
+            if small:
+                totals.append(term)
+            else:
+                left_sum[...] += term
+
+    loop(half, step, small)
+    if small:
+        total = totals[0]
+        for term in totals[1:]:
+            total = total + term
+    else:
+        total = left_sum[...]
+    left_f32[...] = (total.T * (1.0 / rows)).reshape(left_f32.shape)
+    split_parts(lambda place: left_f32[:, place], "narrow", kept_ref, sent_ref)
+
+
+def right_gradient_kernel(sizes, left_keys, *refs):
     rows, channels, copies, _, columns = sizes
-    n_left, n_right = len(left_keys), len(right_keys)
+    n_left = len(left_keys)
     left_refs, refs = list(zip(refs[:n_left], left_keys)), refs[n_left:]
-    right_refs, refs = list(zip(refs[:n_right], right_keys)), refs[n_right:]
-    d_refs, refs = refs[:-8], refs[-8:]
-    left_kept, left_sent, right_kept, right_sent, left_f32, right_f32, left_sum, right_sum = refs
-    place_right(right_refs, right_f32)
+    d_refs, (kept_ref, sent_ref, left_f32, right_sum) = refs[:-4], refs[-4:]
     left_mat = place_left(left_refs, left_f32).astype(jnp.bfloat16)
     pack = LANES // columns
-    scale = 1.0 / rows
     half = channels // pack
     low = lax.broadcasted_iota(jnp.int32, (rows, LANES), 1) < columns
-    small = left_mat.shape[1] <= MXU
 
     def diagonal(outer):
         found = []
@@ -172,21 +208,10 @@
             found.append(total)
         return found
 
-    if not small:
-        left_sum[...] = jnp.zeros_like(left_sum)
-    totals = []
-
     def step(first):
         found = []
-        diag = block_diagonal(right_f32, first, rows, channels, columns, copies)
         for h in range(pack):
-            e = first + h * half
-            d_e = jnp.concatenate([ref[e] for ref in d_refs], axis=0)
-            term = dot(d_e, diag[h], NT)
-            if small:
-                totals.append(term)
-            else:
-                left_sum[...] += term
+            d_e = jnp.concatenate([ref[first + h * half] for ref in d_refs], axis=0)
             found.append(diagonal(dot(left_mat, d_e, NN)))
         if pack == 1:
             result = found[0][0]
@@ -194,27 +219,15 @@
             straight = jnp.where(low, found[0][0], found[1][1])
             crossed = jnp.where(low, found[1][0], found[0][1])
             result = straight + pltpu.roll(crossed, columns, 1)
-        right_sum[pl.ds(first, rows, stride=half), :] = result * scale
-
-    loop(half, step, small)
-    if small:
-        total = totals[0]
-        for term in totals[1:]:
-            total = total + term
-        left_sum[...] = total
-
-    place = lax.axis_index("wide")
-    for n in range(right_kept.shape[0]):
-        count = right_kept.shape[1]
-        for key, ref in ((2 * n, right_kept), (2 * n + 1, right_sent)):
-            start = pl.multiple_of((place ^ key) * count, count)
-            ref[n] = right_sum[pl.ds(start, count), :].astype(ref.dtype)
-    left_f32[...] = (left_sum[...].T * scale).reshape(left_f32.shape)
-    place = lax.axis_index("narrow")
-    for n in range(left_kept.shape[0]):
-        for key, ref in ((2 * n, left_kept), (2 * n + 1, left_sent)):
-            for copy in range(copies):
-                ref[n, copy] = left_f32[copy, place ^ key].astype(ref.dtype)
+        right_sum[pl.ds(first, rows, stride=half), :] = result * (1.0 / rows)
+
+    loop(half, step, left_mat.shape[1] <= MXU)
+    count = kept_ref.shape[1]
+
+    def part(place):
+        return right_sum[pl.ds(pl.multiple_of(place * count, count), count), :]
+
+    split_parts(part, "wide", kept_ref, sent_ref)
 
 
 def forward_kernel(sizes, left_keys, right_keys, *refs):
@@ -340,7 +353,7 @@
 
     hbm = functools.partial(pltpu.with_memory_space_constraint, memory_space=pltpu.HBM)
 
-    steps = powers(n_wide)[1:] + [1]
+    steps = powers(n_wide)[:0:-1] + [1]
     narrow_steps = powers(n_narrow)[::-1]
     right_new = exchange(right, "wide", steps[0])
     source = left
@@ -402,22 +415,19 @@
     left_f32 = pltpu.VMEM((copies, n_narrow, part, groups * channels), f32)
     right_f32 = pltpu.VMEM((rows * channels // pack, LANES), f32)
     far, near = n_narrow // 2, n_wide // 2
-    left_kept, left_sent, right_kept, right_sent = call(
-        functools.partial(gradient_kernel, sizes, left_keys, right_keys),
-        [
-            shape((far,) + left_shape, f32),
-            shape((far,) + left_shape, bf16),
-            shape((near,) + right_shape, f32),
-            shape((near,) + right_shape, bf16),
-        ],
-        [*lefts, *rights, *d_outer],
-        [
-            left_f32,
-            right_f32,
-            pltpu.VMEM((groups * channels, copies * rows), f32),
-            pltpu.VMEM((rows * channels // pack, LANES), f32),
-        ],
-        cost=flops * 2,
+    left_kept, left_sent = call(
+        functools.partial(left_gradient_kernel, sizes, right_keys),
+        [shape((far,) + left_shape, f32), shape((far,) + left_shape, bf16)],
+        [*rights, *d_outer],
+        [left_f32, right_f32, pltpu.VMEM((groups * channels, copies * rows), f32)],
+        cost=flops,
+    )
+    right_kept, right_sent = call(
+        functools.partial(right_gradient_kernel, sizes, left_keys),
+        [shape((near,) + right_shape, f32), shape((near,) + right_shape, bf16)],
+        [*lefts, *d_outer],
+        [left_f32, right_f32],
+        cost=flops,
     )
     left_new = exchange(left_sent, "narrow", 1)
     right_new = exchange(right_sent, "wide", 1)

time: 35.7 us -> 27.7 us (0.78)
  waiting for transfers between devices: 8.44 us -> 2.31 us
  starting transfers between devices: 18.2 us -> 16.1 us
    ppermute x11, waiting for transfers between devices: 8.44 us -> 2.31 us  [exchange(): return lax.ppermute(x, axis, [(n, n ^ m) for n in range(size)])]
    ppermute x11, starting transfers between devices: 18.2 us -> 16.1 us  [exchange(): return lax.ppermute(x, axis, [(n, n ^ m) for n in range(size)])]
    pallas_call x12 -> x13, Pallas kernels: 8.17 us -> 8.38 us  [call(): pl.pallas_call(kernel, in_specs=in_specs or vmem(len(args)), out_specs=ou...]
  transfers between devices with their start and end apart: 11 -> 11, of which waited for: 6 -> 3; matrix products, arithmetic and copies ran while one was open for 0% -> 0% of each run, Pallas kernels for 14% -> 27%
where the time goes in v3:
time: 27.7 us; the launch traced here: 27.6 us
  starting transfers between devices  16.1 us (58%)
  Pallas kernels  8.38 us (30%)
  waiting for transfers between devices  2.31 us (8%)
  between operations  0.76 us (3%)
    ppermute x11, starting transfers between devices, exchange(): return lax.ppermute(x, axis, [(n, n ^ m) for n in range(size)])  16.1 us
    pallas_call x13, Pallas kernels, call(): pl.pallas_call(kernel, in_specs=in_specs or vmem(len(args)), out_specs=ou...  8.38 us
    ppermute x11, waiting for transfers between devices, exchange(): return lax.ppermute(x, axis, [(n, n ^ m) for n in range(size)])  2.31 us
  transfers between devices with their start and end apart: 11, of which 3 were waited for; matrix products, arithmetic and copies ran while one was open for 0% of the time, Pallas kernels for 27%

profile of v3, /device:TPU:0, one launch (start us, length us, event | category | flops | bytes accessed | tf_op | source)
XLA Modules:
  0.0 27.6 jit_solution(6094268167375305701)
XLA Ops:
  0.6 3.1 %collective-permute-start.2 = (bf16[4,32,64]{2,1,0:T(8,128)(2,1)}, bf16[4,32,64]{2,1,0:T(8,128)(2,1)S(1)}, u32[]{:S(2)}, u32[]{:S(2)}) collective-permute-start(bf16[4,32,64]{2,1,0:T(8,128)(2,1)} %refs_1_.1), channel_id=1, source_target_pairs={{0,16},{4,20},{8,24},{12,28},{16,0},{20,4},{24,8},{28,12},{1,17},{... | collective-permute-start | bytes 49160 | tf_op jit(solution)/shard_map/ppermute | solution.py:307
  3.7 1.2 %shard_map.76 = (bf16[1,4,8,256]{3,2,1,0:T(8,128)(2,1)S(1)}, bf16[4,32,64]{2,1,0:T(8,128)(2,1)S(1)}, bf16[1024,128]{1,0:T(8,128)(2,1)S(1)}, bf16[32,64,128]{2,1,0:T(8,128)(2,1)S(1)}) custom-call(bf16[8,32,32]{2,1,0:T(8,128)(2,1)} %refs_0_.1, bf16[4,32,64]{2,1,0:T(8,128)(2,1)} %refs_1_.1, bf16[1024,128]{1,0:T(8,128)(2,1)} %refs_2_.1, bf16[32,64,128]{2,1,0:T(8,128)(2,1)} %refs_3_.1), custom_call_target="tpu_custom_call" | custom-call | flops 33554432 | bytes 65536 | tf_op jit(solution)/shard_map/pallas_call | solution.py:340
  4.9 2.7 %collective-permute-start = (bf16[1,4,8,256]{3,2,1,0:T(8,128)(2,1)S(1)}, bf16[1,4,8,256]{3,2,1,0:T(8,128)(2,1)S(1)}, u32[]{:S(2)}, u32[]{:S(2)}) collective-permute-start(bf16[1,4,8,256]{3,2,1,0:T(8,128)(2,1)S(1)} %get-tuple-element.21.one), channel_id=1, source_target_pairs={{0,2},{1,3},{2,0},{3,1},{4,6},{5,7},{6,4},{7,5},{8,10},{9,11},{10,... | collective-permute-start | bytes 49160 | tf_op jit(solution)/shard_map/ppermute | solution.py:307
  7.6 0.4 %shard_map.77 = (bf16[32,32,128]{2,1,0:T(8,128)(2,1)S(1)}, bf16[128,1024]{1,0:T(8,128)(2,1)S(1)}) custom-call(bf16[1024,128]{1,0:T(8,128)(2,1)S(1)} %get-tuple-element.19.weight_ref), custom_call_target="tpu_custom_call" | custom-call | flops 67108864 | bytes 65536 | tf_op jit(solution)/shard_map/pallas_call | solution.py:340
  8.0 0.7 %shard_map.79.refs_0_.refs_2_ = bf16[32,128,256]{2,1,0:T(8,128)(2,1)S(1)} custom-call(bf16[32,64,128]{2,1,0:T(8,128)(2,1)S(1)} %get-tuple-element.23.cot_ref, bf16[32,32,128]{2,1,0:T(8,128)(2,1)S(1)} %get-tuple-element.24.weight_ref), custom_call_target="tpu_custom_call" | custom-call | flops 268435456 | bytes 65536 | tf_op jit(solution)/shard_map/pallas_call | solution.py:340
  8.7 0.0 collective-permute-done.2.other
  8.7 0.1 shard_map.80.one
  8.8 1.6 %collective-permute-start.3 = (bf16[2,64,128]{2,1,0:T(8,128)(2,1)S(1)}, bf16[2,64,128]{2,1,0:T(8,128)(2,1)S(1)}, u32[]{:S(2)}, u32[]{:S(2)}) collective-permute-start(bf16[2,64,128]{2,1,0:T(8,128)(2,1)S(1)} %shard_map.80.one), channel_id=1, source_target_pairs={{0,8},{4,12},{8,0},{12,4},{16,24},{20,28},{24,16},{28,20},{1,9},{5... | collective-permute-start | bytes 98312 | tf_op jit(solution)/shard_map/ppermute | solution.py:307
  10.3 0.0 collective-permute-done.other
  10.3 1.6 %collective-permute-start.1 = (bf16[2,4,8,256]{3,2,1,0:T(8,128)(2,1)S(1)}, bf16[2,4,8,256]{3,2,1,0:T(8,128)(2,1)S(1)}, u32[]{:S(2)}, u32[]{:S(2)}) collective-permute-start(bf16[2,4,8,256]{3,2,1,0:T(8,128)(2,1)S(1)} %shard_map.78.refs_2_.refs_0_), channel_id=1, source_target_pairs={{0,1},{1,0},{2,3},{3,2},{4,5},{5,4},{6,7},{7,6},{8,9},{9,8},{10,11... | collective-permute-start | bytes 98312 | tf_op jit(solution)/shard_map/ppermute | solution.py:307
  11.9 0.7 %shard_map.81.refs_0_.refs_3_ = bf16[32,128,256]{2,1,0:T(8,128)(2,1)S(1)} custom-call(bf16[32,64,128]{2,1,0:T(8,128)(2,1)S(1)} %get-tuple-element.23.cot_ref, bf16[32,32,128]{2,1,0:T(8,128)(2,1)S(1)} %get-tuple-element.24.weight_ref), custom_call_target="tpu_custom_call" | custom-call | flops 268435456 | bytes 65536 | tf_op jit(solution)/shard_map/pallas_call | solution.py:340
  12.6 0.1 collective-permute-done.3.other
  12.8 0.0 collective-permute-start.4
  12.8 1.5 %collective-permute-done.1.refs_3_.refs_1_ = bf16[2,4,8,256]{3,2,1,0:T(8,128)(2,1)S(1)} collective-permute-done((bf16[2,4,8,256]{3,2,1,0:T(8,128)(2,1)S(1)}, bf16[2,4,8,256]{3,2,1,0:T(8,128)(2,1)S(1)}, u32[]{:S(2)}, u32[]{:S(2)}) %collective-permute-start.1) | collective-permute-done | bytes 32800 | tf_op jit(solution)/shard_map/ppermute | solution.py:307
  14.3 0.8 %shard_map.86 = (f32[4,64,128]{2,1,0:T(8,128)S(1)}, bf16[4,64,128]{2,1,0:T(8,128)(2,1)S(1)}) custom-call(bf16[2,4,8,256]{3,2,1,0:T(8,128)(2,1)S(1)} %shard_map.78.refs_2_.refs_0_, bf16[2,4,8,256]{3,2,1,0:T(8,128)(2,1)S(1)} %collective-permute-done.1.refs_3_.refs_1_, bf16[32,128,256]{2,1,0:T(8,128)(2,1)S(1)} %shard_map.79.refs_0_.refs_2_, ...), custom_call_target="tpu_custom_call" | custom-call | flops 536870912 | bytes 65536 | tf_op jit(solution)/shard_map/pallas_call | solution.py:340
  15.1 0.0 copy-start
  15.1 0.1 collective-permute-start.7
  15.2 0.0 collective-permute-done.4.refs_5_.refs_1_
  15.2 1.4 %shard_map.84 = (f32[2,4,8,256]{3,2,1,0:T(8,128)S(1)}, bf16[2,4,8,256]{3,2,1,0:T(8,128)(2,1)S(1)}) custom-call(bf16[4,64,128]{2,1,0:T(8,128)(2,1)S(1)} %shard_map.82.refs_4_.refs_0_, bf16[4,64,128]{2,1,0:T(8,128)(2,1)S(1)} %collective-permute-done.4.refs_5_.refs_1_, bf16[32,128,256]{2,1,0:T(8,128)(2,1)S(1)} %shard_map.79.refs_0_.refs_2_, ...), custom_call_target="tpu_custom_call" | custom-call | flops 536870912 | bytes 65536 | tf_op jit(solution)/shard_map/pallas_call | solution.py:340
  16.6 1.6 %collective-permute-start.5 = (bf16[2,4,8,256]{3,2,1,0:T(8,128)(2,1)S(1)}, bf16[2,4,8,256]{3,2,1,0:T(8,128)(2,1)S(1)}, u32[]{:S(2)}, u32[]{:S(2)}) collective-permute-start(bf16[2,4,8,256]{3,2,1,0:T(8,128)(2,1)S(1)} %get-tuple-element.26), channel_id=1, source_target_pairs={{0,1},{1,0},{2,3},{3,2},{4,5},{5,4},{6,7},{7,6},{8,9},{9,8},{10,11... | collective-permute-start | bytes 98312 | tf_op jit(solution)/shard_map/ppermute | solution.py:307
  18.2 0.0 collective-permute-done.7.new
  18.3 0.8 %collective-permute-start.10 = (bf16[64,128]{1,0:T(8,128)(2,1)S(1)}, bf16[64,128]{1,0:T(8,128)(2,1)S(1)}, u32[]{:S(2)}, u32[]{:S(2)}) collective-permute-start(bf16[64,128]{1,0:T(8,128)(2,1)S(1)} %get-tuple-element.34), channel_id=1, source_target_pairs={{0,24},{4,28},{8,16},{12,20},{16,8},{20,12},{24,0},{28,4},{1,25},{... | collective-permute-start | bytes 49160 | tf_op jit(solution)/shard_map/ppermute | solution.py:307
  19.1 1.3 %collective-permute-start.8 = (bf16[64,128]{1,0:T(8,128)(2,1)S(1)}, bf16[64,128]{1,0:T(8,128)(2,1)S(1)}, u32[]{:S(2)}, u32[]{:S(2)}) collective-permute-start(bf16[64,128]{1,0:T(8,128)(2,1)S(1)} %get-tuple-element.32), channel_id=1, source_target_pairs={{0,8},{4,12},{8,0},{12,4},{16,24},{20,28},{24,16},{28,20},{1,9},{5... | collective-permute-start | bytes 49160 | tf_op jit(solution)/shard_map/ppermute | solution.py:307
  20.3 1.5 %collective-permute-start.9 = (bf16[64,128]{1,0:T(8,128)(2,1)S(1)}, bf16[64,128]{1,0:T(8,128)(2,1)S(1)}, u32[]{:S(2)}, u32[]{:S(2)}) collective-permute-start(bf16[64,128]{1,0:T(8,128)(2,1)S(1)} %get-tuple-element.33), channel_id=1, source_target_pairs={{0,16},{4,20},{8,24},{12,28},{16,0},{20,4},{24,8},{28,12},{1,17},{... | collective-permute-start | bytes 49160 | tf_op jit(solution)/shard_map/ppermute | solution.py:307
  21.8 0.0 collective-permute-done.5.new
  21.8 2.0 %collective-permute-start.6 = (bf16[4,8,256]{2,1,0:T(8,128)(2,1)S(1)}, bf16[4,8,256]{2,1,0:T(8,128)(2,1)S(1)}, u32[]{:S(2)}, u32[]{:S(2)}) collective-permute-start(bf16[4,8,256]{2,1,0:T(8,128)(2,1)S(1)} %get-tuple-element.28), channel_id=1, source_target_pairs={{0,2},{1,3},{2,0},{3,1},{4,6},{5,7},{6,4},{7,5},{8,10},{9,11},{10,... | collective-permute-start | bytes 49160 | tf_op jit(solution)/shard_map/ppermute | solution.py:307
  23.8 0.0 copy-done
  23.8 2.0 %shard_map.83.pairs = bf16[32,64,128]{2,1,0:T(8,128)(2,1)S(1)} custom-call(bf16[128,1024]{1,0:T(8,128)(2,1)S(1)} %get-tuple-element.20.refs_0_, f32[1,128]{1,0:T(1,128)S(1)} %bitcast.1, bf16[2,4,8,256]{3,2,1,0:T(8,128)(2,1)S(1)} %shard_map.78.refs_2_.refs_0_, bf16[2,4,8,256]{3,2,1,0:T(8,128)(2,1)S(1)} %collective-permute-done.1.refs_3_.refs_1_, ...), custom_call_target="tpu_custom_call" | custom-call | flops 1073741824 | bytes 65536 | tf_op jit(solution)/shard_map/pallas_call | solution.py:340
  25.9 0.0 collective-permute-done.10.refs_5_
  25.9 0.0 collective-permute-done.8.refs_3_
  25.9 0.0 collective-permute-done.9.refs_4_
  25.9 0.7 %collective-permute-done.6.refs_1_ = bf16[4,8,256]{2,1,0:T(8,128)(2,1)S(1)} collective-permute-done((bf16[4,8,256]{2,1,0:T(8,128)(2,1)S(1)}, bf16[4,8,256]{2,1,0:T(8,128)(2,1)S(1)}, u32[]{:S(2)}, u32[]{:S(2)}) %collective-permute-start.6) | collective-permute-done | bytes 16416 | tf_op jit(solution)/shard_map/ppermute | solution.py:307
  26.6 1.0 %shard_map.88 = (bf16[32,64,128]{2,1,0:T(8,128)(2,1)}, f32[8,32,32]{2,1,0:T(8,128)}, f32[4,32,64]{2,1,0:T(8,128)}) custom-call(bf16[32,64,128]{2,1,0:T(8,128)(2,1)S(1)} %shard_map.83.pairs, f32[4,8,256]{2,1,0:T(8,128)S(1)} %get-tuple-element.27.refs_0_, bf16[4,8,256]{2,1,0:T(8,128)(2,1)S(1)} %collective-permute-done.6.refs_1_, ...), custom_call_target="tpu_custom_call" | custom-call | bytes 65536 | tf_op jit(solution)/shard_map/pallas_call | solution.py:340
  (4 shorter events, 0.0 us)
Async XLA Ops:
  0.6 8.0 %collective-permute-start.2 = (bf16[4,32,64]{2,1,0:T(8,128)(2,1)}, bf16[4,32,64]{2,1,0:T(8,128)(2,1)S(1)}, u32[]{:S(2)}, u32[]{:S(2)}) collective-permute-start(bf16[4,32,64]{2,1,0:T(8,128)(2,1)} %refs_1_.1), channel_id=1, source_target_pairs={{0,16},{4,20},{8,24},{12,28},{16,0},{20,4},{24,8},{28,12},{1,17},{... | collective-permute-start | bytes 49160 | tf_op jit(solution)/shard_map/ppermute | solution.py:307
  4.9 5.4 %collective-permute-start = (bf16[1,4,8,256]{3,2,1,0:T(8,128)(2,1)S(1)}, bf16[1,4,8,256]{3,2,1,0:T(8,128)(2,1)S(1)}, u32[]{:S(2)}, u32[]{:S(2)}) collective-permute-start(bf16[1,4,8,256]{3,2,1,0:T(8,128)(2,1)S(1)} %get-tuple-element.21.one), channel_id=1, source_target_pairs={{0,2},{1,3},{2,0},{3,1},{4,6},{5,7},{6,4},{7,5},{8,10},{9,11},{10,... | collective-permute-start | bytes 49160 | tf_op jit(solution)/shard_map/ppermute | solution.py:307
  8.8 4.0 %collective-permute-start.3 = (bf16[2,64,128]{2,1,0:T(8,128)(2,1)S(1)}, bf16[2,64,128]{2,1,0:T(8,128)(2,1)S(1)}, u32[]{:S(2)}, u32[]{:S(2)}) collective-permute-start(bf16[2,64,128]{2,1,0:T(8,128)(2,1)S(1)} %shard_map.80.one), channel_id=1, source_target_pairs={{0,8},{4,12},{8,0},{12,4},{16,24},{20,28},{24,16},{28,20},{1,9},{5... | collective-permute-start | bytes 98312 | tf_op jit(solution)/shard_map/ppermute | solution.py:307
  10.3 3.9 %collective-permute-start.1 = (bf16[2,4,8,256]{3,2,1,0:T(8,128)(2,1)S(1)}, bf16[2,4,8,256]{3,2,1,0:T(8,128)(2,1)S(1)}, u32[]{:S(2)}, u32[]{:S(2)}) collective-permute-start(bf16[2,4,8,256]{3,2,1,0:T(8,128)(2,1)S(1)} %shard_map.78.refs_2_.refs_0_), channel_id=1, source_target_pairs={{0,1},{1,0},{2,3},{3,2},{4,5},{5,4},{6,7},{7,6},{8,9},{9,8},{10,11... | collective-permute-start | bytes 98312 | tf_op jit(solution)/shard_map/ppermute | solution.py:307
  12.8 2.4 %collective-permute-start.4 = (bf16[4,64,128]{2,1,0:T(8,128)(2,1)S(1)}, bf16[4,64,128]{2,1,0:T(8,128)(2,1)S(1)}, u32[]{:S(2)}, u32[]{:S(2)}) collective-permute-start(bf16[4,64,128]{2,1,0:T(8,128)(2,1)S(1)} %shard_map.82.refs_4_.refs_0_), channel_id=1, source_target_pairs={{0,4},{4,0},{8,12},{12,8},{16,20},{20,16},{24,28},{28,24},{1,5},{5... | collective-permute-start | bytes 196616 | tf_op jit(solution)/shard_map/ppermute | solution.py:307
  15.1 8.8 %copy-start = (f32[128]{0:T(128)S(1)}, f32[128]{0:T(128)}, u32[]{:S(2)}) copy-start(f32[128]{0:T(128)} %param.8) | copy-start | bytes 1540
  15.1 3.2 %collective-permute-start.7 = (bf16[4,64,128]{2,1,0:T(8,128)(2,1)S(1)}, bf16[4,64,128]{2,1,0:T(8,128)(2,1)S(1)}, u32[]{:S(2)}, u32[]{:S(2)}) collective-permute-start(bf16[4,64,128]{2,1,0:T(8,128)(2,1)S(1)} %get-tuple-element.30), channel_id=1, source_target_pairs={{0,4},{4,0},{8,12},{12,8},{16,20},{20,16},{24,28},{28,24},{1,5},{5... | collective-permute-start | bytes 196616 | tf_op jit(solution)/shard_map/ppermute | solution.py:307
  16.6 5.2 %collective-permute-start.5 = (bf16[2,4,8,256]{3,2,1,0:T(8,128)(2,1)S(1)}, bf16[2,4,8,256]{3,2,1,0:T(8,128)(2,1)S(1)}, u32[]{:S(2)}, u32[]{:S(2)}) collective-permute-start(bf16[2,4,8,256]{3,2,1,0:T(8,128)(2,1)S(1)} %get-tuple-element.26), channel_id=1, source_target_pairs={{0,1},{1,0},{2,3},{3,2},{4,5},{5,4},{6,7},{7,6},{8,9},{9,8},{10,11... | collective-permute-start | bytes 98312 | tf_op jit(solution)/shard_map/ppermute | solution.py:307
  18.3 7.6 %collective-permute-start.10 = (bf16[64,128]{1,0:T(8,128)(2,1)S(1)}, bf16[64,128]{1,0:T(8,128)(2,1)S(1)}, u32[]{:S(2)}, u32[]{:S(2)}) collective-permute-start(bf16[64,128]{1,0:T(8,128)(2,1)S(1)} %get-tuple-element.34), channel_id=1, source_target_pairs={{0,24},{4,28},{8,16},{12,20},{16,8},{20,12},{24,0},{28,4},{1,25},{... | collective-permute-start | bytes 49160 | tf_op jit(solution)/shard_map/ppermute | solution.py:307
  19.1 6.9 %collective-permute-start.8 = (bf16[64,128]{1,0:T(8,128)(2,1)S(1)}, bf16[64,128]{1,0:T(8,128)(2,1)S(1)}, u32[]{:S(2)}, u32[]{:S(2)}) collective-permute-start(bf16[64,128]{1,0:T(8,128)(2,1)S(1)} %get-tuple-element.32), channel_id=1, source_target_pairs={{0,8},{4,12},{8,0},{12,4},{16,24},{20,28},{24,16},{28,20},{1,9},{5... | collective-permute-start | bytes 49160 | tf_op jit(solution)/shard_map/ppermute | solution.py:307
  20.3 5.6 %collective-permute-start.9 = (bf16[64,128]{1,0:T(8,128)(2,1)S(1)}, bf16[64,128]{1,0:T(8,128)(2,1)S(1)}, u32[]{:S(2)}, u32[]{:S(2)}) collective-permute-start(bf16[64,128]{1,0:T(8,128)(2,1)S(1)} %get-tuple-element.33), channel_id=1, source_target_pairs={{0,16},{4,20},{8,24},{12,28},{16,0},{20,4},{24,8},{28,12},{1,17},{... | collective-permute-start | bytes 49160 | tf_op jit(solution)/shard_map/ppermute | solution.py:307
  21.8 4.8 %collective-permute-start.6 = (bf16[4,8,256]{2,1,0:T(8,128)(2,1)S(1)}, bf16[4,8,256]{2,1,0:T(8,128)(2,1)S(1)}, u32[]{:S(2)}, u32[]{:S(2)}) collective-permute-start(bf16[4,8,256]{2,1,0:T(8,128)(2,1)S(1)} %get-tuple-element.28), channel_id=1, source_target_pairs={{0,2},{1,3},{2,0},{3,1},{4,6},{5,7},{6,4},{7,5},{8,10},{9,11},{10,... | collective-permute-start | bytes 49160 | tf_op jit(solution)/shard_map/ppermute | solution.py:307

commit v4 on v3

--- a/solution.py
+++ b/solution.py
@@ -148,9 +148,11 @@
 
 def split_parts(total, axis, kept_ref, sent_ref):
     place = lax.axis_index(axis)
-    for n in range(kept_ref.shape[0]):
-        kept_ref[n] = total(place ^ (2 * n)).astype(kept_ref.dtype)
-        sent_ref[n] = total(place ^ (2 * n + 1)).astype(sent_ref.dtype)
+    count = kept_ref.shape[0]
+    for n in range(count):
+        keys = (n, n + count) if axis == "narrow" else (2 * n, 2 * n + 1)
+        kept_ref[n] = total(place ^ keys[0]).astype(kept_ref.dtype)
+        sent_ref[n] = total(place ^ keys[1]).astype(sent_ref.dtype)
 
 
 def left_gradient_kernel(sizes, right_keys, *refs):
@@ -399,7 +401,7 @@
         new = [k ^ m for k in keys]
         if n + 1 < len(steps):
             change = dense if n == 0 else None
-            rights = stack(rights, right_new, change, d_outer[n : n + 1])
+            rights = stack(rights, right_new, change, d_outer[:1])
             keys = keys + new
     right_keys, rights = (keys, new), [rights, right_new]
 
@@ -429,7 +431,7 @@
         [left_f32, right_f32],
         cost=flops,
     )
-    left_new = exchange(left_sent, "narrow", 1)
+    left_new = exchange(left_sent, "narrow", far)
     right_new = exchange(right_sent, "wide", 1)
 
     def add(kept, new):
@@ -441,7 +443,7 @@
         right_sums[n] = exchange(right_sums[n], "wide", 2 * n)
     left_sums = add(left_kept, left_new)
     for n in range(1, far):
-        left_sums[n] = exchange(left_sums[n], "narrow", 2 * n)
+        left_sums[n] = exchange(left_sums[n], "narrow", n)
 
     (pairs,) = call(
         functools.partial(forward_kernel, sizes, left_keys, right_keys),

time: 27.7 us -> 30 us (1.083)
  waiting for transfers between devices: 2.31 us -> 3.62 us
  starting transfers between devices: 16.1 us -> 17.1 us
    ppermute x11, waiting for transfers between devices: 2.31 us -> 3.62 us  [exchange(): return lax.ppermute(x, axis, [(n, n ^ m) for n in range(size)])]
    ppermute x11, starting transfers between devices: 16.1 us -> 17.1 us  [exchange(): return lax.ppermute(x, axis, [(n, n ^ m) for n in range(size)])]
  transfers between devices with their start and end apart: 11 -> 11, of which waited for: 3 -> 2; matrix products, arithmetic and copies ran while one was open for 0% -> 0% of each run, Pallas kernels for 27% -> 25%
where the time goes in v4:
time: 30 us; the launch traced here: 29.9 us
  starting transfers between devices  17.1 us (57%)
  Pallas kernels  8.38 us (28%)
  waiting for transfers between devices  3.62 us (12%)
  between operations  0.77 us (3%)
    ppermute x11, starting transfers between devices, exchange(): return lax.ppermute(x, axis, [(n, n ^ m) for n in range(size)])  17.1 us
    pallas_call x13, Pallas kernels, call(): pl.pallas_call(kernel, in_specs=in_specs or vmem(len(args)), out_specs=ou...  8.38 us
    ppermute x11, waiting for transfers between devices, exchange(): return lax.ppermute(x, axis, [(n, n ^ m) for n in range(size)])  3.62 us
  transfers between devices with their start and end apart: 11, of which 2 were waited for; matrix products, arithmetic and copies ran while one was open for 0% of the time, Pallas kernels for 25%

profile of v4, /device:TPU:0, one launch (start us, length us, event | category | flops | bytes accessed | tf_op | source)
XLA Modules:
  0.0 29.9 jit_solution(15545489238488162994)
XLA Ops:
  0.6 3.1 %collective-permute-start.2 = (bf16[4,32,64]{2,1,0:T(8,128)(2,1)}, bf16[4,32,64]{2,1,0:T(8,128)(2,1)S(1)}, u32[]{:S(2)}, u32[]{:S(2)}) collective-permute-start(bf16[4,32,64]{2,1,0:T(8,128)(2,1)} %refs_1_.1), channel_id=1, source_target_pairs={{0,16},{4,20},{8,24},{12,28},{16,0},{20,4},{24,8},{28,12},{1,17},{... | collective-permute-start | bytes 49160 | tf_op jit(solution)/shard_map/ppermute | solution.py:309
  3.7 1.2 %shard_map.76 = (bf16[1,4,8,256]{3,2,1,0:T(8,128)(2,1)S(1)}, bf16[4,32,64]{2,1,0:T(8,128)(2,1)S(1)}, bf16[1024,128]{1,0:T(8,128)(2,1)S(1)}, bf16[32,64,128]{2,1,0:T(8,128)(2,1)S(1)}) custom-call(bf16[8,32,32]{2,1,0:T(8,128)(2,1)} %refs_0_.1, bf16[4,32,64]{2,1,0:T(8,128)(2,1)} %refs_1_.1, bf16[1024,128]{1,0:T(8,128)(2,1)} %refs_2_.1, bf16[32,64,128]{2,1,0:T(8,128)(2,1)} %refs_3_.1), custom_call_target="tpu_custom_call" | custom-call | flops 33554432 | bytes 65536 | tf_op jit(solution)/shard_map/pallas_call | solution.py:342
  4.9 0.4 %shard_map.77 = (bf16[32,32,128]{2,1,0:T(8,128)(2,1)S(1)}, bf16[128,1024]{1,0:T(8,128)(2,1)S(1)}) custom-call(bf16[1024,128]{1,0:T(8,128)(2,1)S(1)} %get-tuple-element.19.weight_ref), custom_call_target="tpu_custom_call" | custom-call | flops 67108864 | bytes 65536 | tf_op jit(solution)/shard_map/pallas_call | solution.py:342
  5.3 0.7 %shard_map.79.refs_0_.refs_2_ = bf16[32,128,256]{2,1,0:T(8,128)(2,1)S(1)} custom-call(bf16[32,64,128]{2,1,0:T(8,128)(2,1)S(1)} %get-tuple-element.23.cot_ref, bf16[32,32,128]{2,1,0:T(8,128)(2,1)S(1)} %get-tuple-element.24.weight_ref), custom_call_target="tpu_custom_call" | custom-call | flops 268435456 | bytes 65536 | tf_op jit(solution)/shard_map/pallas_call | solution.py:342
  6.0 0.0 collective-permute-done.2.other
  6.0 0.1 shard_map.80.one
  6.1 1.8 %collective-permute-start.3 = (bf16[2,64,128]{2,1,0:T(8,128)(2,1)S(1)}, bf16[2,64,128]{2,1,0:T(8,128)(2,1)S(1)}, u32[]{:S(2)}, u32[]{:S(2)}) collective-permute-start(bf16[2,64,128]{2,1,0:T(8,128)(2,1)S(1)} %shard_map.80.one), channel_id=1, source_target_pairs={{0,8},{4,12},{8,0},{12,4},{16,24},{20,28},{24,16},{28,20},{1,9},{5... | collective-permute-start | bytes 98312 | tf_op jit(solution)/shard_map/ppermute | solution.py:309
  7.9 2.6 %collective-permute-start = (bf16[1,4,8,256]{3,2,1,0:T(8,128)(2,1)S(1)}, bf16[1,4,8,256]{3,2,1,0:T(8,128)(2,1)S(1)}, u32[]{:S(2)}, u32[]{:S(2)}) collective-permute-start(bf16[1,4,8,256]{3,2,1,0:T(8,128)(2,1)S(1)} %get-tuple-element.21.one), channel_id=1, source_target_pairs={{0,2},{1,3},{2,0},{3,1},{4,6},{5,7},{6,4},{7,5},{8,10},{9,11},{10,... | collective-permute-start | bytes 49160 | tf_op jit(solution)/shard_map/ppermute | solution.py:309
  10.5 2.0 %collective-permute-done.other = bf16[1,4,8,256]{3,2,1,0:T(8,128)(2,1)S(1)} collective-permute-done((bf16[1,4,8,256]{3,2,1,0:T(8,128)(2,1)S(1)}, bf16[1,4,8,256]{3,2,1,0:T(8,128)(2,1)S(1)}, u32[]{:S(2)}, u32[]{:S(2)}) %collective-permute-start) | collective-permute-done | bytes 16416 | tf_op jit(solution)/shard_map/ppermute | solution.py:309
  12.6 1.6 %collective-permute-start.1 = (bf16[2,4,8,256]{3,2,1,0:T(8,128)(2,1)S(1)}, bf16[2,4,8,256]{3,2,1,0:T(8,128)(2,1)S(1)}, u32[]{:S(2)}, u32[]{:S(2)}) collective-permute-start(bf16[2,4,8,256]{3,2,1,0:T(8,128)(2,1)S(1)} %shard_map.78.refs_2_.refs_0_), channel_id=1, source_target_pairs={{0,1},{1,0},{2,3},{3,2},{4,5},{5,4},{6,7},{7,6},{8,9},{9,8},{10,11... | collective-permute-start | bytes 98312 | tf_op jit(solution)/shard_map/ppermute | solution.py:309
  14.2 0.0 collective-permute-done.3.other
  14.2 0.1 collective-permute-start.4
  14.2 0.7 %shard_map.83.refs_3_ = bf16[32,128,256]{2,1,0:T(8,128)(2,1)S(1)} custom-call(bf16[32,64,128]{2,1,0:T(8,128)(2,1)S(1)} %get-tuple-element.23.cot_ref, bf16[32,32,128]{2,1,0:T(8,128)(2,1)S(1)} %get-tuple-element.24.weight_ref), custom_call_target="tpu_custom_call" | custom-call | flops 268435456 | bytes 65536 | tf_op jit(solution)/shard_map/pallas_call | solution.py:342
  15.0 1.5 %collective-permute-done.1.refs_3_.refs_1_ = bf16[2,4,8,256]{3,2,1,0:T(8,128)(2,1)S(1)} collective-permute-done((bf16[2,4,8,256]{3,2,1,0:T(8,128)(2,1)S(1)}, bf16[2,4,8,256]{3,2,1,0:T(8,128)(2,1)S(1)}, u32[]{:S(2)}, u32[]{:S(2)}) %collective-permute-start.1) | collective-permute-done | bytes 32800 | tf_op jit(solution)/shard_map/ppermute | solution.py:309
  16.5 0.8 %shard_map.86 = (f32[4,64,128]{2,1,0:T(8,128)S(1)}, bf16[4,64,128]{2,1,0:T(8,128)(2,1)S(1)}) custom-call(bf16[2,4,8,256]{3,2,1,0:T(8,128)(2,1)S(1)} %shard_map.78.refs_2_.refs_0_, bf16[2,4,8,256]{3,2,1,0:T(8,128)(2,1)S(1)} %collective-permute-done.1.refs_3_.refs_1_, bf16[32,128,256]{2,1,0:T(8,128)(2,1)S(1)} %shard_map.79.refs_0_.refs_2_, ...), custom_call_target="tpu_custom_call" | custom-call | flops 536870912 | bytes 65536 | tf_op jit(solution)/shard_map/pallas_call | solution.py:342
  17.3 0.0 copy-start
  17.3 0.1 collective-permute-start.7
  17.4 0.0 collective-permute-done.4.refs_5_.refs_1_
  17.4 1.4 %shard_map.84 = (f32[2,4,8,256]{3,2,1,0:T(8,128)S(1)}, bf16[2,4,8,256]{3,2,1,0:T(8,128)(2,1)S(1)}) custom-call(bf16[4,64,128]{2,1,0:T(8,128)(2,1)S(1)} %shard_map.81.refs_4_.refs_0_, bf16[4,64,128]{2,1,0:T(8,128)(2,1)S(1)} %collective-permute-done.4.refs_5_.refs_1_, bf16[32,128,256]{2,1,0:T(8,128)(2,1)S(1)} %shard_map.79.refs_0_.refs_2_, ...), custom_call_target="tpu_custom_call" | custom-call | flops 536870912 | bytes 65536 | tf_op jit(solution)/shard_map/pallas_call | solution.py:342
  18.9 2.7 %collective-permute-start.5 = (bf16[2,4,8,256]{3,2,1,0:T(8,128)(2,1)S(1)}, bf16[2,4,8,256]{3,2,1,0:T(8,128)(2,1)S(1)}, u32[]{:S(2)}, u32[]{:S(2)}) collective-permute-start(bf16[2,4,8,256]{3,2,1,0:T(8,128)(2,1)S(1)} %get-tuple-element.26), channel_id=1, source_target_pairs={{0,2},{1,3},{2,0},{3,1},{4,6},{5,7},{6,4},{7,5},{8,10},{9,11},{10,... | collective-permute-start | bytes 98312 | tf_op jit(solution)/shard_map/ppermute | solution.py:309
  21.5 0.0 collective-permute-done.7.new
  21.5 1.7 %collective-permute-start.10 = (bf16[64,128]{1,0:T(8,128)(2,1)S(1)}, bf16[64,128]{1,0:T(8,128)(2,1)S(1)}, u32[]{:S(2)}, u32[]{:S(2)}) collective-permute-start(bf16[64,128]{1,0:T(8,128)(2,1)S(1)} %get-tuple-element.34), channel_id=1, source_target_pairs={{0,24},{4,28},{8,16},{12,20},{16,8},{20,12},{24,0},{28,4},{1,25},{... | collective-permute-start | bytes 49160 | tf_op jit(solution)/shard_map/ppermute | solution.py:309
  23.3 1.5 %collective-permute-start.8 = (bf16[64,128]{1,0:T(8,128)(2,1)S(1)}, bf16[64,128]{1,0:T(8,128)(2,1)S(1)}, u32[]{:S(2)}, u32[]{:S(2)}) collective-permute-start(bf16[64,128]{1,0:T(8,128)(2,1)S(1)} %get-tuple-element.32), channel_id=1, source_target_pairs={{0,8},{4,12},{8,0},{12,4},{16,24},{20,28},{24,16},{28,20},{1,9},{5... | collective-permute-start | bytes 49160 | tf_op jit(solution)/shard_map/ppermute | solution.py:309
  24.8 0.3 %collective-permute-start.9 = (bf16[64,128]{1,0:T(8,128)(2,1)S(1)}, bf16[64,128]{1,0:T(8,128)(2,1)S(1)}, u32[]{:S(2)}, u32[]{:S(2)}) collective-permute-start(bf16[64,128]{1,0:T(8,128)(2,1)S(1)} %get-tuple-element.33), channel_id=1, source_target_pairs={{0,16},{4,20},{8,24},{12,28},{16,0},{20,4},{24,8},{28,12},{1,17},{... | collective-permute-start | bytes 49160 | tf_op jit(solution)/shard_map/ppermute | solution.py:309
  25.1 0.0 collective-permute-done.5.new
  25.1 1.7 %collective-permute-start.6 = (bf16[4,8,256]{2,1,0:T(8,128)(2,1)S(1)}, bf16[4,8,256]{2,1,0:T(8,128)(2,1)S(1)}, u32[]{:S(2)}, u32[]{:S(2)}) collective-permute-start(bf16[4,8,256]{2,1,0:T(8,128)(2,1)S(1)} %get-tuple-element.28), channel_id=1, source_target_pairs={{0,1},{1,0},{2,3},{3,2},{4,5},{5,4},{6,7},{7,6},{8,9},{9,8},{10,11... | collective-permute-start | bytes 49160 | tf_op jit(solution)/shard_map/ppermute | solution.py:309
  26.8 0.0 copy-done
  26.8 2.0 %shard_map.82.pairs = bf16[32,64,128]{2,1,0:T(8,128)(2,1)S(1)} custom-call(bf16[128,1024]{1,0:T(8,128)(2,1)S(1)} %get-tuple-element.20.refs_0_, f32[1,128]{1,0:T(1,128)S(1)} %bitcast.1, bf16[2,4,8,256]{3,2,1,0:T(8,128)(2,1)S(1)} %shard_map.78.refs_2_.refs_0_, bf16[2,4,8,256]{3,2,1,0:T(8,128)(2,1)S(1)} %collective-permute-done.1.refs_3_.refs_1_, ...), custom_call_target="tpu_custom_call" | custom-call | flops 1073741824 | bytes 65536 | tf_op jit(solution)/shard_map/pallas_call | solution.py:342
  28.9 0.0 collective-permute-done.10.refs_5_
  28.9 0.0 collective-permute-done.8.refs_3_
  28.9 0.0 collective-permute-done.9.refs_4_
  28.9 0.0 collective-permute-done.6.refs_1_
  28.9 1.0 %shard_map.88 = (bf16[32,64,128]{2,1,0:T(8,128)(2,1)}, f32[8,32,32]{2,1,0:T(8,128)}, f32[4,32,64]{2,1,0:T(8,128)}) custom-call(bf16[32,64,128]{2,1,0:T(8,128)(2,1)S(1)} %shard_map.82.pairs, f32[4,8,256]{2,1,0:T(8,128)S(1)} %get-tuple-element.27.refs_0_, bf16[4,8,256]{2,1,0:T(8,128)(2,1)S(1)} %collective-permute-done.6.refs_1_, ...), custom_call_target="tpu_custom_call" | custom-call | bytes 65536 | tf_op jit(solution)/shard_map/pallas_call | solution.py:342
  (4 shorter events, 0.0 us)
Async XLA Ops:
  0.6 5.4 %collective-permute-start.2 = (bf16[4,32,64]{2,1,0:T(8,128)(2,1)}, bf16[4,32,64]{2,1,0:T(8,128)(2,1)S(1)}, u32[]{:S(2)}, u32[]{:S(2)}) collective-permute-start(bf16[4,32,64]{2,1,0:T(8,128)(2,1)} %refs_1_.1), channel_id=1, source_target_pairs={{0,16},{4,20},{8,24},{12,28},{16,0},{20,4},{24,8},{28,12},{1,17},{... | collective-permute-start | bytes 49160 | tf_op jit(solution)/shard_map/ppermute | solution.py:309
  6.1 8.0 %collective-permute-start.3 = (bf16[2,64,128]{2,1,0:T(8,128)(2,1)S(1)}, bf16[2,64,128]{2,1,0:T(8,128)(2,1)S(1)}, u32[]{:S(2)}, u32[]{:S(2)}) collective-permute-start(bf16[2,64,128]{2,1,0:T(8,128)(2,1)S(1)} %shard_map.80.one), channel_id=1, source_target_pairs={{0,8},{4,12},{8,0},{12,4},{16,24},{20,28},{24,16},{28,20},{1,9},{5... | collective-permute-start | bytes 98312 | tf_op jit(solution)/shard_map/ppermute | solution.py:309
  7.9 4.6 %collective-permute-start = (bf16[1,4,8,256]{3,2,1,0:T(8,128)(2,1)S(1)}, bf16[1,4,8,256]{3,2,1,0:T(8,128)(2,1)S(1)}, u32[]{:S(2)}, u32[]{:S(2)}) collective-permute-start(bf16[1,4,8,256]{3,2,1,0:T(8,128)(2,1)S(1)} %get-tuple-element.21.one), channel_id=1, source_target_pairs={{0,2},{1,3},{2,0},{3,1},{4,6},{5,7},{6,4},{7,5},{8,10},{9,11},{10,... | collective-permute-start | bytes 49160 | tf_op jit(solution)/shard_map/ppermute | solution.py:309
  12.6 3.9 %collective-permute-start.1 = (bf16[2,4,8,256]{3,2,1,0:T(8,128)(2,1)S(1)}, bf16[2,4,8,256]{3,2,1,0:T(8,128)(2,1)S(1)}, u32[]{:S(2)}, u32[]{:S(2)}) collective-permute-start(bf16[2,4,8,256]{3,2,1,0:T(8,128)(2,1)S(1)} %shard_map.78.refs_2_.refs_0_), channel_id=1, source_target_pairs={{0,1},{1,0},{2,3},{3,2},{4,5},{5,4},{6,7},{7,6},{8,9},{9,8},{10,11... | collective-permute-start | bytes 98312 | tf_op jit(solution)/shard_map/ppermute | solution.py:309
  14.2 3.2 %collective-permute-start.4 = (bf16[4,64,128]{2,1,0:T(8,128)(2,1)S(1)}, bf16[4,64,128]{2,1,0:T(8,128)(2,1)S(1)}, u32[]{:S(2)}, u32[]{:S(2)}) collective-permute-start(bf16[4,64,128]{2,1,0:T(8,128)(2,1)S(1)} %shard_map.81.refs_4_.refs_0_), channel_id=1, source_target_pairs={{0,4},{4,0},{8,12},{12,8},{16,20},{20,16},{24,28},{28,24},{1,5},{5... | collective-permute-start | bytes 196616 | tf_op jit(solution)/shard_map/ppermute | solution.py:309
  17.3 9.5 %copy-start = (f32[128]{0:T(128)S(1)}, f32[128]{0:T(128)}, u32[]{:S(2)}) copy-start(f32[128]{0:T(128)} %param.8) | copy-start | bytes 1540
  17.3 4.2 %collective-permute-start.7 = (bf16[4,64,128]{2,1,0:T(8,128)(2,1)S(1)}, bf16[4,64,128]{2,1,0:T(8,128)(2,1)S(1)}, u32[]{:S(2)}, u32[]{:S(2)}) collective-permute-start(bf16[4,64,128]{2,1,0:T(8,128)(2,1)S(1)} %get-tuple-element.30), channel_id=1, source_target_pairs={{0,4},{4,0},{8,12},{12,8},{16,20},{20,16},{24,28},{28,24},{1,5},{5... | collective-permute-start | bytes 196616 | tf_op jit(solution)/shard_map/ppermute | solution.py:309
  18.9 6.2 %collective-permute-start.5 = (bf16[2,4,8,256]{3,2,1,0:T(8,128)(2,1)S(1)}, bf16[2,4,8,256]{3,2,1,0:T(8,128)(2,1)S(1)}, u32[]{:S(2)}, u32[]{:S(2)}) collective-permute-start(bf16[2,4,8,256]{3,2,1,0:T(8,128)(2,1)S(1)} %get-tuple-element.26), channel_id=1, source_target_pairs={{0,2},{1,3},{2,0},{3,1},{4,6},{5,7},{6,4},{7,5},{8,10},{9,11},{10,... | collective-permute-start | bytes 98312 | tf_op jit(solution)/shard_map/ppermute | solution.py:309
  21.5 7.3 %collective-permute-start.10 = (bf16[64,128]{1,0:T(8,128)(2,1)S(1)}, bf16[64,128]{1,0:T(8,128)(2,1)S(1)}, u32[]{:S(2)}, u32[]{:S(2)}) collective-permute-start(bf16[64,128]{1,0:T(8,128)(2,1)S(1)} %get-tuple-element.34), channel_id=1, source_target_pairs={{0,24},{4,28},{8,16},{12,20},{16,8},{20,12},{24,0},{28,4},{1,25},{... | collective-permute-start | bytes 49160 | tf_op jit(solution)/shard_map/ppermute | solution.py:309
  23.3 5.6 %collective-permute-start.8 = (bf16[64,128]{1,0:T(8,128)(2,1)S(1)}, bf16[64,128]{1,0:T(8,128)(2,1)S(1)}, u32[]{:S(2)}, u32[]{:S(2)}) collective-permute-start(bf16[64,128]{1,0:T(8,128)(2,1)S(1)} %get-tuple-element.32), channel_id=1, source_target_pairs={{0,8},{4,12},{8,0},{12,4},{16,24},{20,28},{24,16},{28,20},{1,9},{5... | collective-permute-start | bytes 49160 | tf_op jit(solution)/shard_map/ppermute | solution.py:309
  24.8 4.1 %collective-permute-start.9 = (bf16[64,128]{1,0:T(8,128)(2,1)S(1)}, bf16[64,128]{1,0:T(8,128)(2,1)S(1)}, u32[]{:S(2)}, u32[]{:S(2)}) collective-permute-start(bf16[64,128]{1,0:T(8,128)(2,1)S(1)} %get-tuple-element.33), channel_id=1, source_target_pairs={{0,16},{4,20},{8,24},{12,28},{16,0},{20,4},{24,8},{28,12},{1,17},{... | collective-permute-start | bytes 49160 | tf_op jit(solution)/shard_map/ppermute | solution.py:309
  25.1 3.8 %collective-permute-start.6 = (bf16[4,8,256]{2,1,0:T(8,128)(2,1)S(1)}, bf16[4,8,256]{2,1,0:T(8,128)(2,1)S(1)}, u32[]{:S(2)}, u32[]{:S(2)}) collective-permute-start(bf16[4,8,256]{2,1,0:T(8,128)(2,1)S(1)} %get-tuple-element.28), channel_id=1, source_target_pairs={{0,1},{1,0},{2,3},{3,2},{4,5},{5,4},{6,7},{7,6},{8,9},{9,8},{10,11... | collective-permute-start | bytes 49160 | tf_op jit(solution)/shard_map/ppermute | solution.py:309
